TPU v7x, 256 devices: a whole 4x4x8 slice. The times are simulated.
256 devices in a mesh: rows: 32 (over y, z), cols: 8 (over x, core).
Axes of the slice: x: 4, y: 4, z: 8, core: 2. Of those that a mesh axis runs over, the one named last changes fastest.
Arguments:
- sketches: bfloat16 [8192, 16384], P('rows', 'cols'), may hold values from -6 to 6, as said below
- start_basis: bfloat16 [16384, 256], P('cols'), may hold values from -6 to 6
- shrink_index: int32 [1], replicated, may hold values from 64 to 191
Outputs:
- shrunk: float32 [256, 16384], P('rows', 'cols')
Inputs may be any that keep to these rules, and one draw needn't show every extreme that they name: `sketches`: real entries.
All inputs are finite; a program needn't handle non-finite values.
Results may differ from a plain program's by a relative error of at most 0.0028.
Values may be sent and summed in bfloat16 or wider, within the bound.
No kernel may reach another device: no remote copies, remote signals or barrier semaphores. Data moves between devices by JAX's collectives and lax.ppermute only.
A program may use at most 64 MiB of HBM per device.

v0:
```python
import jax
import jax.numpy as jnp
from jax import lax
from jax.sharding import PartitionSpec as P

ITERS = 3


def copy_for_each(x, axis):
    copies = jnp.broadcast_to(x, (lax.axis_size(axis), *x.shape))
    return lax.all_to_all(copies, axis, split_axis=0, concat_axis=0, tiled=True)


def of_everyone(x, axis):
    everything = copy_for_each(x, axis)
    return jnp.sum(everything, axis=0)


def over_pieces(x, axis):
    blocks = lax.all_gather(x, axis)
    return blocks.sum(axis=0)


def project(sketches, basis_bf):
    partial_product = jnp.dot(sketches, basis_bf, preferred_element_type=jnp.float32)
    return of_everyone(partial_product, "cols")


def orthonormal(images, gram_total):
    lower_factor = jnp.linalg.cholesky(gram_total)
    return jax.scipy.linalg.solve_triangular(lower_factor, images.T, lower=True).T


def body(sketches, start_basis, shrink_index):
    basis_bf = start_basis
    basis = start_basis.astype(jnp.float32)
    for loop_index in range(ITERS):
        projected_bf = project(sketches, basis_bf).astype(jnp.bfloat16)
        local_images = jnp.einsum(
            "lw,lk->wk", sketches, projected_bf, preferred_element_type=jnp.float32
        )
        images = lax.psum(local_images, "rows")
        gram_total = over_pieces(jnp.dot(images.T, images, precision=lax.Precision.HIGHEST), "cols")
        basis = orthonormal(images, gram_total)
        basis_bf = basis.astype(jnp.bfloat16)
    projected = project(sketches, basis_bf)
    energy = of_everyone(jnp.sum(projected * projected, axis=0), "rows")
    ordered = jnp.sort(energy)[::-1]
    threshold = lax.dynamic_index_in_dim(ordered, shrink_index[0], 0, keepdims=False)
    factor = jnp.sqrt(jnp.maximum(energy - threshold, 0.25 * threshold))
    owned_rows = basis.shape[1] // lax.axis_size("rows")
    offset = lax.axis_index("rows") * owned_rows
    columns = lax.dynamic_slice_in_dim(basis, offset, owned_rows, 1)
    scaled = columns * lax.dynamic_slice_in_dim(factor, offset, owned_rows, 0)[None, :]
    return scaled.T


def solution(mesh):
    return jax.shard_map(
        body,
        mesh=mesh,
        in_specs=(P("rows", "cols"), P("cols", None), P()),
        out_specs=P("rows", "cols"),
        check_vma=False,
    )
```

profile of v0, /device:TPU:1, one launch (start us, length us, event | category | flops | bytes accessed | tf_op | source)
XLA Modules:
  0.0 945.3 jit_solution(6524417354252199078)
XLA Ops:
  11.0 6.7 all-to-all-start
  17.7 26.2 %all-to-all-done = f32[8,256,256]{2,1,0:T(8,128)S(1)} async-done(((f32[8,256,256]{2,1,0:T(8,128)}), f32[8,256,256]{2,1,0:T(8,128)S(1)}, u32[]{:S(2)}, u32[]{:S(2)}) %all-to-all-start) | async-done | bytes 2097184 | tf_op jit(solution)/shard_map/all_to_all | solution.py:11
  45.8 150.7 %all-reduce.5.cloned.1.call-done = f32[2048,256]{0,1:T(8,128)} async-done(((f32[2048,256]{0,1:T(8,128)}), f32[2048,256]{0,1:T(8,128)}) %all-reduce.5.cloned.1.call-update) | async-done | bytes 2097168 | tf_op jit(solution)/shard_map/psum | solution.py:42
  196.6 4.8 fusion.46
  201.9 29.3 %all-gather.7.cloned.1.call-done = f32[2048,256]{1,0:T(8,128)} async-done(((f32[256,256]{1,0:T(8,128)}), f32[2048,256]{1,0:T(8,128)}) %all-gather.7.cloned.1.call-update) | async-done | bytes 2097168 | tf_op jit(solution)/shard_map/all_gather | solution.py:20
  235.6 11.7 %cholesky.172 = f32[128,128]{1,0:T(8,128)S(1)} custom-call(f32[128,128]{1,0:T(8,128)S(1)} %cholesky.270), custom_call_target="Cholesky" | custom-call | tf_op jit(solution)/shard_map/jit(cholesky)/cholesky | solution.py:30
  247.3 9.8 %custom-call.15 = f32[1,128,128]{1,2,0:T(8,128)S(1)} custom-call(f32[1,128,128]{2,1,0:T(8,128)S(1)} %get-tuple-element.74), custom_call_target="InvertDiagBlocksLowerTriangular" | custom-call | tf_op jit(solution)/shard_map/jit(cholesky)/cholesky | solution.py:30
  259.4 11.7 %cholesky.189 = f32[128,128]{1,0:T(8,128)S(1)} custom-call(f32[128,128]{1,0:T(8,128)S(1)} %convolution_subtract_fusion.5), custom_call_target="Cholesky" | custom-call | tf_op jit(solution)/shard_map/jit(cholesky)/cholesky | solution.py:30
  274.0 4.0 while.6
  278.7 20.5 %custom-call.16 = f32[2,128,128]{1,2,0:T(8,128)S(1)} custom-call(f32[2,128,128]{2,1,0:T(8,128)} %copy-done.12), custom_call_target="InvertDiagBlocksLowerTriangular" | custom-call | tf_op jit(solution)/shard_map/jit(_solve_triangular)/triangular_solve | solution.py:31
  303.2 29.6 %all_to_all.26 = f32[8,256,256]{2,1,0:T(8,128)S(1)} all-to-all(f32[8,256,256]{2,1,0:T(8,128)S(1)} %broadcast_in_dim.18), channel_id=1, replica_groups=mesh['rows'=32,'cols'=8] {'cols'}, dimensions={0} | all-to-all | bytes 4194304 | tf_op jit(solution)/shard_map/all_to_all | solution.py:11
  334.8 150.2 %all-reduce.7.cloned.1.call-done = f32[2048,256]{0,1:T(8,128)} async-done(((f32[2048,256]{0,1:T(8,128)}), f32[2048,256]{0,1:T(8,128)}) %all-reduce.7.cloned.1.call-update) | async-done | bytes 2097168 | tf_op jit(solution)/shard_map/psum | solution.py:42
  485.0 4.8 fusion.47
  490.0 29.6 %all-gather.9.cloned.1.call-done = f32[2048,256]{1,0:T(8,128)} async-done(((f32[256,256]{1,0:T(8,128)}), f32[2048,256]{1,0:T(8,128)}) %all-gather.9.cloned.1.call-update) | async-done | bytes 2097168 | tf_op jit(solution)/shard_map/all_gather | solution.py:20
  524.0 11.7 %cholesky.206 = f32[128,128]{1,0:T(8,128)S(1)} custom-call(f32[128,128]{1,0:T(8,128)S(1)} %cholesky.273), custom_call_target="Cholesky" | custom-call | tf_op jit(solution)/shard_map/jit(cholesky)/cholesky | solution.py:30
  535.8 9.8 %custom-call.17 = f32[1,128,128]{1,2,0:T(8,128)S(1)} custom-call(f32[1,128,128]{2,1,0:T(8,128)S(1)} %get-tuple-element.70), custom_call_target="InvertDiagBlocksLowerTriangular" | custom-call | tf_op jit(solution)/shard_map/jit(cholesky)/cholesky | solution.py:30
  547.8 11.7 %cholesky.223 = f32[128,128]{1,0:T(8,128)S(1)} custom-call(f32[128,128]{1,0:T(8,128)S(1)} %convolution_subtract_fusion.4), custom_call_target="Cholesky" | custom-call | tf_op jit(solution)/shard_map/jit(cholesky)/cholesky | solution.py:30
  563.0 4.3 while.7
  567.9 20.5 %custom-call.18 = f32[2,128,128]{1,2,0:T(8,128)S(1)} custom-call(f32[2,128,128]{2,1,0:T(8,128)} %copy-done.13), custom_call_target="InvertDiagBlocksLowerTriangular" | custom-call | tf_op jit(solution)/shard_map/jit(_solve_triangular)/triangular_solve | solution.py:31
  592.4 29.6 %all_to_all.27 = f32[8,256,256]{2,1,0:T(8,128)S(1)} all-to-all(f32[8,256,256]{2,1,0:T(8,128)S(1)} %broadcast_in_dim.19), channel_id=1, replica_groups=mesh['rows'=32,'cols'=8] {'cols'}, dimensions={0} | all-to-all | bytes 4194304 | tf_op jit(solution)/shard_map/all_to_all | solution.py:11
  624.2 150.0 %all-reduce.9.cloned.1.call-done = f32[2048,256]{0,1:T(8,128)} async-done(((f32[2048,256]{0,1:T(8,128)}), f32[2048,256]{0,1:T(8,128)}) %all-reduce.9.cloned.1.call-update) | async-done | bytes 2097168 | tf_op jit(solution)/shard_map/psum | solution.py:42
  774.2 4.8 fusion.48
  779.0 29.9 %all-gather.11.cloned.1.call-done = f32[2048,256]{1,0:T(8,128)} async-done(((f32[256,256]{1,0:T(8,128)}), f32[2048,256]{1,0:T(8,128)}) %all-gather.11.cloned.1.call-update) | async-done | bytes 2097168 | tf_op jit(solution)/shard_map/all_gather | solution.py:20
  813.2 11.7 %cholesky.240 = f32[128,128]{1,0:T(8,128)S(1)} custom-call(f32[128,128]{1,0:T(8,128)S(1)} %cholesky.276), custom_call_target="Cholesky" | custom-call | tf_op jit(solution)/shard_map/jit(cholesky)/cholesky | solution.py:30
  825.0 9.8 %custom-call.19 = f32[1,128,128]{1,2,0:T(8,128)S(1)} custom-call(f32[1,128,128]{2,1,0:T(8,128)S(1)} %get-tuple-element.66), custom_call_target="InvertDiagBlocksLowerTriangular" | custom-call | tf_op jit(solution)/shard_map/jit(cholesky)/cholesky | solution.py:30
  837.0 11.9 %cholesky.257 = f32[128,128]{1,0:T(8,128)S(1)} custom-call(f32[128,128]{1,0:T(8,128)S(1)} %convolution_subtract_fusion.3), custom_call_target="Cholesky" | custom-call | tf_op jit(solution)/shard_map/jit(cholesky)/cholesky | solution.py:30
  852.4 3.9 while.8
  857.0 20.5 %custom-call.20 = f32[2,128,128]{1,2,0:T(8,128)S(1)} custom-call(f32[2,128,128]{2,1,0:T(8,128)} %copy-done.14), custom_call_target="InvertDiagBlocksLowerTriangular" | custom-call | tf_op jit(solution)/shard_map/jit(_solve_triangular)/triangular_solve | solution.py:31
  881.5 29.7 %all_to_all.28 = f32[8,256,256]{2,1,0:T(8,128)} all-to-all(f32[8,256,256]{2,1,0:T(8,128)S(1)} %broadcast_in_dim.20), channel_id=1, replica_groups=mesh['rows'=32,'cols'=8] {'cols'}, dimensions={0} | all-to-all | bytes 4194304 | tf_op jit(solution)/shard_map/all_to_all | solution.py:11
  913.7 9.6 %all-to-all-start.4 = ((f32[32,1,256]{2,1,0:T(1,128)}), f32[32,1,256]{2,1,0:T(1,128)S(1)}, u32[]{:S(2)}, u32[]{:S(2)}) async-start(f32[32,1,256]{2,1,0:T(1,128)} %broadcast_in_dim.21), calls=%async_computation.4 | async-start | bytes 65536 | tf_op jit(solution)/shard_map/all_to_all | solution.py:11
  924.0 8.1 all-to-all-done.4
  932.1 3.3 sort.15
  (136 shorter events, 67.1 us)
Async XLA Ops:
  6.5 1.2 copy-start
  11.0 32.9 %all-to-all-start = ((f32[8,256,256]{2,1,0:T(8,128)}), f32[8,256,256]{2,1,0:T(8,128)S(1)}, u32[]{:S(2)}, u32[]{:S(2)}) async-start(f32[8,256,256]{2,1,0:T(8,128)} %broadcast_in_dim.17), calls=%async_computation | async-start | bytes 4194304 | tf_op jit(solution)/shard_map/all_to_all | solution.py:11
  17.7 178.9 %all-reduce.5.cloned.1.call-start = ((), (), s32[]{:S(2)}) async-start(), calls=%async_computation.5 | async-start | bytes 4194304 | tf_op jit(solution)/shard_map/psum | solution.py:42
  45.8 185.5 %all-gather.7.cloned.1.call-start = ((), (), s32[]{:S(2)}) async-start(), calls=%async_computation.8 | async-start | bytes 2359296 | tf_op jit(solution)/shard_map/all_gather | solution.py:20
  201.4 283.6 %all-reduce.7.cloned.1.call-start = ((), (), s32[]{:S(2)}) async-start(), calls=%async_computation.6 | async-start | bytes 4194304 | tf_op jit(solution)/shard_map/psum | solution.py:42
  233.0 66.2 %copy-start.1 = (f32[2048,256]{0,1:T(8,128)S(1)}, f32[2048,256]{0,1:T(8,128)}, u32[]{:S(2)}) copy-start(f32[2048,256]{0,1:T(8,128)} %all-reduce.5.cloned.1.call-done) | copy-start | bytes 6291460
  234.9 0.7 copy-start.9
  271.1 1.8 copy-start.8
  278.1 0.7 copy-start.12
  334.8 184.9 %all-gather.9.cloned.1.call-start = ((), (), s32[]{:S(2)}) async-start(), calls=%async_computation.9 | async-start | bytes 2359296 | tf_op jit(solution)/shard_map/all_gather | solution.py:20
  489.8 284.4 %all-reduce.9.cloned.1.call-start = ((), (), s32[]{:S(2)}) async-start(), calls=%async_computation.7 | async-start | bytes 4194304 | tf_op jit(solution)/shard_map/psum | solution.py:42
  521.4 67.0 %copy-start.2 = (f32[2048,256]{0,1:T(8,128)S(1)}, f32[2048,256]{0,1:T(8,128)}, u32[]{:S(2)}) copy-start(f32[2048,256]{0,1:T(8,128)} %all-reduce.7.cloned.1.call-done) | copy-start | bytes 6291460
  523.3 0.7 copy-start.10
  559.5 2.5 copy-start.6
  567.3 0.7 copy-start.13
  623.9 185.0 %all-gather.11.cloned.1.call-start = ((), (), s32[]{:S(2)}) async-start(), calls=%async_computation.10 | async-start | bytes 2359296 | tf_op jit(solution)/shard_map/all_gather | solution.py:20
  810.7 66.8 %copy-start.3 = (f32[2048,256]{0,1:T(8,128)S(1)}, f32[2048,256]{0,1:T(8,128)}, u32[]{:S(2)}) copy-start(f32[2048,256]{0,1:T(8,128)} %all-reduce.9.cloned.1.call-done) | copy-start | bytes 6291460
  812.5 0.7 copy-start.11
  848.9 2.5 copy-start.7
  856.3 0.7 copy-start.14
  878.5 2.1 copy-start.4
  911.2 26.3 %copy-start.5 = (f32[128,2048]{1,0:T(8,128)S(1)}, f32[128,2048]{1,0:T(8,128)}, u32[]{:S(2)}) copy-start(f32[128,2048]{1,0:T(8,128)} %copy-done.4) | copy-start | bytes 3145732
  913.7 18.4 %all-to-all-start.4 = ((f32[32,1,256]{2,1,0:T(1,128)}), f32[32,1,256]{2,1,0:T(1,128)S(1)}, u32[]{:S(2)}, u32[]{:S(2)}) async-start(f32[32,1,256]{2,1,0:T(1,128)} %broadcast_in_dim.21), calls=%async_computation.4 | async-start | bytes 65536 | tf_op jit(solution)/shard_map/all_to_all | solution.py:11
Sparse Core Ops, SparseCore 0:
  45.9 150.5 all-reduce.4
  201.5 29.7 all-gather.6
  334.9 150.0 all-reduce.6
  489.9 29.7 all-gather.8
  624.1 150.0 all-reduce.8
  779.1 29.7 all-gather.10
where the time goes:
time: 950 us; the launch traced here: 945 us
  waiting for transfers between devices  574 us (60%)
  other arithmetic  183 us (19%)
  blocking collectives  89 us (9%)
  matrix products  38.6 us (4%)
  local copies, waits for them, and re-layouts  23.4 us (2%)
  between operations  19.1 us (2%)
  starting transfers between devices  17.4 us (2%)
    psum x3, waiting for transfers between devices, body(): images = lax.psum(local_images, 'rows')  451 us
    another operation x20, other arithmetic, orthonormal(): lower_factor = jnp.linalg.cholesky(gram_total)  103 us
    all_to_all x3, blocking collectives, copy_for_each(): return lax.all_to_all(copies, axis, split_axis=0, concat_axis=0, tiled=True)  89 us
    all_gather x3, waiting for transfers between devices, over_pieces(): blocks = lax.all_gather(x, axis)  88.9 us
    another operation x7, other arithmetic, orthonormal(): jax.scipy.linalg.solve_triangular(lower_factor, images.T, lower=True)  64.4 us
    all_to_all x2, waiting for transfers between devices, copy_for_each(): return lax.all_to_all(copies, axis, split_axis=0, concat_axis=0, tiled=True)  34.4 us
  transfers between devices with their start and end apart: 8, of which 8 were waited for; matrix products, arithmetic and copies ran while one was open for 0% of the time, Pallas kernels for 0%

commit v1 on v0

v1 whole, which is shorter than its diff:
```python
import jax
import jax.numpy as jnp
from jax import lax
from jax.experimental import pallas as pl
from jax.experimental.pallas import tpu as pltpu
from jax.sharding import Mesh, PartitionSpec as P

ITERS = 3
f32 = jnp.float32
bf16 = jnp.bfloat16
HI = lax.Precision.HIGHEST
VMEM = pl.BlockSpec(memory_space=pltpu.VMEM)
L = 256
PANEL = 32
LANES = 128


def vmem(shape, dtype=f32):
    return pltpu.VMEM(shape, dtype)


def near(*arrays):
    return tuple(pltpu.with_memory_space_constraint(x, pltpu.VMEM) for x in arrays)


def limit(mib):
    return pltpu.CompilerParams(vmem_limit_bytes=mib << 20)


def tdot(a, b):
    return lax.dot_general(a, b, (((0,), (0,)), ((), ())), precision=HI, preferred_element_type=f32)


def factor_inverse(g_ref, b_ref, w_ref, x_ref):
    sub = lax.broadcasted_iota(jnp.int32, (8, LANES), 0)
    lane = lax.broadcasted_iota(jnp.int32, (8, LANES), 1)
    groups = PANEL // 8
    b_ref[:, 0:L] = g_ref[0:LANES, :]
    b_ref[:, L:] = jnp.zeros((LANES, LANES), f32)

    def half(step, carry):
        for k in range(LANES // PANEL):
            c0 = k * PANEL
            base = b_ref[c0 : c0 + PANEL, :]
            if k > 0:
                base = base - tdot(w_ref[0:c0, c0 : c0 + PANEL], w_ref[0:c0, :])
            a = [[base[8 * q : 8 * q + 8, LANES * t : LANES * (t + 1)] for t in range(3)] for q in range(groups)]
            for q in range(groups):
                a[q][2] = a[q][2] + jnp.where(lane == sub + (c0 + 8 * q), 1.0, 0.0).astype(f32)
            for p in range(0, groups, 2):
                c = c0 + 8 * p
                col = [
                    {q: jnp.broadcast_to(a[q][0][:, c + i : c + i + 1], (8, LANES)) for q in range(p, groups)}
                    for i in range(16)
                ]
                for j in range(16):
                    h, r = p + j // 8, j % 8
                    below = range(h, groups)
                    inv = lax.rsqrt(jnp.broadcast_to(col[j][h][r : r + 1, :], (8, LANES)))
                    m = {q: col[j][q] * inv for q in below}
                    m[h] = jnp.where(sub > r, m[h], 0.0)
                    row = [jnp.broadcast_to(a[h][t][r : r + 1, :], (8, LANES)) * inv for t in range(3)]
                    for i in range(j + 1, 16):
                        ci = jnp.broadcast_to(col[i][h][r : r + 1, :], (8, LANES)) * inv
                        for q in below:
                            col[i][q] = col[i][q] - m[q] * ci
                    for q in below:
                        for t in range(3):
                            a[q][t] = a[q][t] - m[q] * row[t]
                    for t in range(3):
                        a[h][t] = jnp.where(sub == r, row[t], a[h][t])
            for q in range(groups):
                for t in range(3):
                    w_ref[c0 + 8 * q : c0 + 8 * q + 8, LANES * t : LANES * (t + 1)] = a[q][t]

        @pl.when(step == 0)
        def _():
            x_ref[0:LANES, 0:LANES] = w_ref[:, L:]
            x_ref[0:LANES, LANES:L] = jnp.zeros((LANES, LANES), f32)
            u = tdot(w_ref[:, LANES:L], w_ref[:, LANES:])
            b_ref[:, 0:LANES] = g_ref[LANES:L, LANES:L] - u[:, :LANES]
            b_ref[:, LANES:L] = -u[:, LANES:]

        @pl.when(step == 1)
        def _():
            x_ref[LANES:L, :] = w_ref[:, LANES:]

        return carry

    lax.fori_loop(0, 2, half, 0)


def step_kernel(s_ref, p_ref, x_ref, w_ref, b_ref, g_ref):
    for d in range(16):
        g_ref[16 * d : 16 * d + 16, :] = s_ref[d, 0:16, :]
    factor_inverse(g_ref, b_ref, w_ref, x_ref)
    for n in range(2):
        t = jnp.concatenate([s_ref[8 * n + d, 16:48, :] for d in range(8)], axis=0)
        p_ref[256 * n : 256 * n + 256, :] = lax.dot_general(
            t, x_ref[...], (((1,), (1,)), ((), ())), precision=HI, preferred_element_type=f32
        ).astype(p_ref.dtype)


def factor_step(s, last):
    shared = [vmem((LANES, 3 * LANES)), vmem((LANES, 3 * LANES)), vmem((L, L))]
    inverse = vmem((L, L))
    projected = vmem((512, L), f32 if last else bf16)
    return pl.pallas_call(
        step_kernel,
        out_shape=(projected, inverse) if last else projected,
        in_specs=[VMEM],
        out_specs=(VMEM, VMEM) if last else VMEM,
        scratch_shapes=shared if last else [inverse, *shared],
        compiler_params=limit(12),
        name="factor_step",
    )(*near(s))


def split(v):
    a = v.astype(bf16)
    r = v - a.astype(f32)
    b = r.astype(bf16)
    return a, b, (r - b.astype(f32)).astype(bf16)


def products_kernel(s_ref, i_ref, *refs):
    o_ref = refs[-1]
    i = i_ref[...]
    t = sum(jnp.dot(s_ref[...], part, preferred_element_type=f32) for part in split(i))
    g = tdot(i, i)
    for d in range(16):
        both = jnp.concatenate([g[16 * d : 16 * d + 16, :], t[32 * d : 32 * d + 32, :]], axis=0)
        o_ref[d] = both if len(refs) == 1 else both + refs[0][d]


def products(s, i, *add):
    return pl.pallas_call(
        products_kernel,
        out_shape=vmem((16, 48, L)),
        in_specs=[VMEM] * (2 + len(add)),
        out_specs=VMEM,
        compiler_params=limit(16),
        name="products",
    )(*near(s, i, *add))


def finish_kernel(n_ref, e_ref, a_ref, b_ref, o_ref, t_ref):
    e = e_ref[0]
    for d in range(1, 8):
        e = e + e_ref[d]
    across = jnp.broadcast_to(e, (L, L))
    t_ref[...] = jnp.transpose(across)
    down = t_ref[...]
    k = n_ref[0]
    above = jnp.sum((across > down).astype(jnp.int32), axis=1, keepdims=True)
    least = jnp.sum((across >= down).astype(jnp.int32), axis=1, keepdims=True)
    at_k = (above <= k) & (k < least)
    threshold = jnp.max(jnp.where(at_k, down[:, 0:1], -jnp.inf), axis=0, keepdims=True)
    mine = t_ref[pl.ds(pl.multiple_of(n_ref[1] * 8, 8), 8), 0:1]
    factor = jnp.sqrt(jnp.maximum(mine - threshold, 0.25 * threshold))
    odd = n_ref[2] == 1
    a = a_ref[...] * factor
    b = b_ref[...] * factor
    o_ref[:, 0:1024] = jnp.where(odd, b, a)
    o_ref[:, 1024:2048] = jnp.where(odd, a, b)


def finish(scalars, energies, a, b):
    return pl.pallas_call(
        finish_kernel,
        out_shape=jax.ShapeDtypeStruct((8, 2048), f32),
        in_specs=[pl.BlockSpec(memory_space=pltpu.SMEM)] + [VMEM] * 3,
        out_specs=VMEM,
        scratch_shapes=[pltpu.VMEM((L, L), f32)],
        compiler_params=limit(8),
        name="finish",
    )(scalars, *near(energies, a, b))


def gather(x, axis, n):
    return lax.all_to_all(jnp.broadcast_to(x, (n, *x.shape)), axis, 0, 0, tiled=True)


def scatter_sum(x, axis):
    return jnp.sum(lax.all_to_all(x, axis, 0, 0, tiled=True).astype(f32), axis=0)


def swap(x):
    return lax.ppermute(x, "c", [(0, 1), (1, 0)])


def body(sketches, start_basis, shrink_index):
    y, z, c = lax.axis_index("y"), lax.axis_index("z"), lax.axis_index("c")
    parts = []
    for k in (0, 1):
        half = lax.dynamic_slice_in_dim(sketches, ((y + k) % 2) * 1024, 1024, 1)
        pairs = [(2 * v + d, 2 * (2 * d + (v + k) % 2) + v // 2) for v in range(4) for d in range(2)]
        parts.append(lax.ppermute(half, ("y", "c"), pairs))
    odd = y % 2 == 1
    s = jnp.concatenate([jnp.where(odd, parts[1], parts[0]), jnp.where(odd, parts[0], parts[1])], axis=0)
    s_own = lax.dynamic_slice_in_dim(s, c * 512, 512, 1)
    s_oth = lax.dynamic_slice_in_dim(s, (1 - c) * 512, 512, 1)

    t = jnp.dot(sketches, start_basis, preferred_element_type=f32)
    chunk = scatter_sum(t.reshape(8, 32, L), ("x", "c")).astype(bf16)
    rows = gather(chunk, ("x", "c"), 8).reshape(256, L)
    same = lax.ppermute(rows, ("y", "c"), [(2 * v + d, 2 * (2 * (v % 2) + d) + v // 2) for v in range(4) for d in range(2)])
    flip = lax.ppermute(rows, ("y", "c"), [(2 * v + d, 2 * (2 * (1 - v % 2) + d) + v // 2) for v in range(4) for d in range(2)])
    upper = y // 2 == 1
    projected = jnp.concatenate([jnp.where(upper, flip, same), jnp.where(upper, same, flip)], axis=0)
    for it in range(ITERS):
        def images(part):
            return lax.dot_general(part, projected, (((0,), (0,)), ((), ())), preferred_element_type=f32)

        half = images(s_own) + swap(images(s_oth).astype(bf16)).astype(f32)
        chunk = scatter_sum(half.astype(bf16).reshape(8, 64, L), "z")
        i_own = gather(chunk, "z", 8).reshape(512, L)
        i_oth = swap(i_own)
        both = products(s_oth, i_oth, products(s_own, i_own))
        sums = scatter_sum(both, ("x", "y"))
        whole = gather(sums, ("x", "y"), 16)
        if it < ITERS - 1:
            projected = factor_step(whole, False)
    projected, inverse = factor_step(whole, True)
    partial = jnp.sum(projected * projected, axis=0, keepdims=True)
    partial = partial + swap(partial)
    energies = gather(partial, "z", 8)
    rows = jnp.concatenate(
        [lax.dynamic_slice_in_dim(inverse, 8 * ((2 * c + (y + k) % 2) * 8 + z), 8, 0) for k in (0, 1)], axis=0
    )
    own, oth = (
        lax.dot_general(rows, i, (((1,), (1,)), ((), ())), precision=HI, preferred_element_type=f32)
        for i in (i_own, i_oth)
    )
    basis = jnp.where(c == 0, jnp.concatenate([own, oth], axis=1), jnp.concatenate([oth, own], axis=1))
    out = []
    for k in (0, 1):
        pairs = [(2 * v + d, 2 * (2 * d + (v + k) % 2) + v // 2) for v in range(4) for d in range(2)]
        out.append(lax.ppermute(basis[8 * k : 8 * k + 8], ("y", "c"), pairs))
    scalars = jnp.stack([shrink_index[0], y * 8 + z, y % 2]).astype(jnp.int32)
    return finish(scalars, energies, *out)


def solution(mesh):
    grid = Mesh(mesh.devices.reshape(4, 8, 4, 2), ("y", "z", "x", "c"))
    rows, cols = ("y", "z"), ("x", "c")
    return jax.shard_map(
        body,
        mesh=grid,
        in_specs=(P(rows, cols), P(cols, None), P()),
        out_specs=P(rows, cols),
        check_vma=False,
    )
```

time: 950 us -> 310 us (0.33)
  waiting for transfers between devices: 574 us -> 29.3 us
  other arithmetic: 183 us -> 0.68 us
  blocking collectives: 89 us -> 196 us
  matrix products: 38.6 us -> 5.48 us
  Pallas kernels: 0 us -> 32 us
  starting transfers between devices: 17.4 us -> 42.2 us
  local copies, waits for them, and re-layouts: 23.4 us -> 3.14 us
  between operations: 19.1 us -> 0.99 us
    psum x3 -> x0, waiting for transfers between devices: 451 us -> none  [body(): images = lax.psum(local_images, 'rows')]
    another operation x27 -> x1, other arithmetic: 168 us -> 0.08 us  [body(): scalars = jnp.stack([shrink_index[0], y * 8 + z, y % 2]).astype(jnp.int32)]
    all_to_all x3 -> x12, blocking collectives: 89 us -> 196 us  [the longest x6 98.5 us: scatter_sum(): lax.all_to_all(x, axis, 0, 0, tiled=True).astype(f32)]
    all_gather x3 -> x0, waiting for transfers between devices: 88.9 us -> none  [over_pieces(): blocks = lax.all_gather(x, axis)]
    pallas_call x0 -> x10, Pallas kernels: none -> 32 us  [the longest x3 24.2 us: factor_step(): pl.pallas_call(step_kernel, out_shape=(projected, inverse) if last else p...]
    ppermute x0 -> x13, starting transfers between devices: none -> 28.5 us  [the longest x7 14.2 us: swap(): return lax.ppermute(x, 'c', [(0, 1), (1, 0)])]
    dot_general x10 -> x9, matrix products: 22.7 us -> 5.48 us  [the longest x1 2.35 us: body(): t = jnp.dot(sketches, start_basis, preferred_element_type=f32)]
    another operation x15 -> x0, matrix products: 15.8 us -> none  [the longest x9 9.37 us: orthonormal(): jax.scipy.linalg.solve_triangular(lower_factor, images.T, lower=True)]
  transfers between devices with their start and end apart: 8 -> 16, of which waited for: 8 -> 11; matrix products, arithmetic and copies ran while one was open for 0% -> 1% of each run, Pallas kernels for 0% -> 1%
where the time goes in v1:
time: 310 us; the launch traced here: 309 us
  blocking collectives  196 us (63%)
  starting transfers between devices  42.2 us (14%)
  Pallas kernels  32 us (10%)
  waiting for transfers between devices  29.3 us (9%)
  matrix products  5.48 us (2%)
  local copies, waits for them, and re-layouts  3.14 us (1%)
    all_to_all x6, blocking collectives, scatter_sum(): lax.all_to_all(x, axis, 0, 0, tiled=True).astype(f32)  98.5 us
    all_to_all x6, blocking collectives, gather(): lax.all_to_all(jnp.broadcast_to(x, (n, *x.shape)), axis, 0, 0, tiled=True)  97.1 us
    pallas_call x3, Pallas kernels, factor_step(): pl.pallas_call(step_kernel, out_shape=(projected, inverse) if last else p...  24.2 us
    all_to_all x2, waiting for transfers between devices, gather(): lax.all_to_all(jnp.broadcast_to(x, (n, *x.shape)), axis, 0, 0, tiled=True)  18.1 us
    ppermute x7, starting transfers between devices, swap(): return lax.ppermute(x, 'c', [(0, 1), (1, 0)])  14.2 us
    all_to_all x2, starting transfers between devices, gather(): lax.all_to_all(jnp.broadcast_to(x, (n, *x.shape)), axis, 0, 0, tiled=True)  7.17 us
    all_to_all x1, starting transfers between devices, scatter_sum(): lax.all_to_all(x, axis, 0, 0, tiled=True).astype(f32)  6.51 us
  transfers between devices with their start and end apart: 16, of which 11 were waited for; matrix products, arithmetic and copies ran while one was open for 1% of the time, Pallas kernels for 1%

profile of v1, /device:TPU:1, one launch (start us, length us, event | category | flops | bytes accessed | tf_op | source)
XLA Modules:
  0.0 309.3 jit_solution(11910636360215449055)
XLA Ops:
  1.2 2.4 fusion.12
  3.6 6.5 %all-to-all-start = ((f32[8,32,256]{2,1,0:T(8,128)}), f32[8,32,256]{2,1,0:T(8,128)S(1)}, u32[]{:S(2)}, u32[]{:S(2)}) async-start(f32[8,32,256]{2,1,0:T(8,128)} %bitcast.2), calls=%async_computation | async-start | bytes 524288 | tf_op jit(solution)/shard_map/all_to_all | solution.py:185
  10.2 4.0 %collective-permute-start.1 = (bf16[256,1024]{1,0:T(8,128)(2,1)S(1)}, bf16[256,1024]{1,0:T(8,128)(2,1)S(1)}, u32[]{:S(2)}, u32[]{:S(2)}) collective-permute-start(bf16[256,1024]{1,0:T(8,128)(2,1)S(1)} %get-tuple-element.13), channel_id=1, source_target_pairs={{0,0},{1,128},{64,64},{65,192},{128,1},{129,129},{192,65},{193,193... | collective-permute-start | bytes 1572872 | tf_op jit(solution)/shard_map/ppermute | solution.py:198
  16.6 8.7 %all_to_all.75 = bf16[8,32,256]{2,1,0:T(8,128)(2,1)S(1)} all-to-all(bf16[8,32,256]{2,1,0:T(8,128)(2,1)S(1)} %broadcast_in_dim.27), channel_id=1, replica_groups=mesh['y'=4,'z'=8,'x'=4,'c'=2] {'x','c'}, dimensions={0} | all-to-all | bytes 262144 | tf_op jit(solution)/shard_map/all_to_all | solution.py:181
  25.3 3.2 %collective-permute-start.3 = (bf16[256,256]{1,0:T(8,128)(2,1)S(1)}, bf16[256,256]{1,0:T(8,128)(2,1)S(1)}, u32[]{:S(2)}, u32[]{:S(2)}) collective-permute-start(bf16[256,256]{1,0:T(8,128)(2,1)S(1)} %bitcast.36), channel_id=1, source_target_pairs={{0,0},{1,64},{64,128},{65,192},{128,1},{129,65},{192,129},{193,193... | collective-permute-start | bytes 393224 | tf_op jit(solution)/shard_map/ppermute | solution.py:207
  28.5 1.5 collective-permute-start.2
  30.0 3.4 %collective-permute-done.3 = bf16[256,256]{1,0:T(8,128)(2,1)S(1)} collective-permute-done((bf16[256,256]{1,0:T(8,128)(2,1)S(1)}, bf16[256,256]{1,0:T(8,128)(2,1)S(1)}, u32[]{:S(2)}, u32[]{:S(2)}) %collective-permute-start.3) | collective-permute-done | bytes 131104 | tf_op jit(solution)/shard_map/ppermute | solution.py:207
  35.6 1.5 collective-permute-done.4
  37.4 20.2 %all_to_all.76 = bf16[8,64,256]{2,1,0:T(8,128)(2,1)S(1)} all-to-all(bf16[8,64,256]{2,1,0:T(8,128)(2,1)S(1)} %bitcast.33), channel_id=1, replica_groups=mesh['y'=4,'z'=8,'x'=4,'c'=2] {'z'}, dimensions={0} | all-to-all | bytes 524288 | tf_op jit(solution)/shard_map/all_to_all | solution.py:185
  57.7 19.7 %all_to_all.77 = f32[8,64,256]{2,1,0:T(8,128)S(1)} all-to-all(f32[8,64,256]{2,1,0:T(8,128)S(1)} %broadcast_in_dim.28), channel_id=1, replica_groups=mesh['y'=4,'z'=8,'x'=4,'c'=2] {'z'}, dimensions={0} | all-to-all | bytes 1048576 | tf_op jit(solution)/shard_map/all_to_all | solution.py:181
  81.1 16.2 %all_to_all.78 = f32[16,48,256]{2,1,0:T(8,128)S(1)} all-to-all(f32[16,48,256]{2,1,0:T(8,128)S(1)} %products.7), channel_id=1, replica_groups=mesh['y'=4,'z'=8,'x'=4,'c'=2] {'x','y'}, dimensions={0} | all-to-all | bytes 1572864 | tf_op jit(solution)/shard_map/all_to_all | solution.py:185
  97.5 15.1 %all_to_all.79.s_ref = f32[16,48,256]{2,1,0:T(8,128)S(1)} all-to-all(f32[16,48,256]{2,1,0:T(8,128)S(1)} %broadcast_in_dim.29), channel_id=1, replica_groups=mesh['y'=4,'z'=8,'x'=4,'c'=2] {'x','y'}, dimensions={0} | all-to-all | bytes 1572864 | tf_op jit(solution)/shard_map/all_to_all | solution.py:181
  112.6 8.1 %factor_step.3 = bf16[512,256]{1,0:T(8,128)(2,1)S(1)} custom-call(f32[16,48,256]{2,1,0:T(8,128)S(1)} %all_to_all.79.s_ref), custom_call_target="tpu_custom_call" | custom-call | tf_op jit(solution)/shard_map/factor_step/pallas_call | solution.py:108
  121.0 3.5 %collective-permute-start.6 = (bf16[512,256]{1,0:T(8,128)(2,1)S(1)}, bf16[512,256]{1,0:T(8,128)(2,1)S(1)}, u32[]{:S(2)}, u32[]{:S(2)}) collective-permute-start(bf16[512,256]{1,0:T(8,128)(2,1)S(1)} %convolution_convert_fusion.1), channel_id=1, source_target_pairs={{0,1},{1,0},{2,3},{3,2},{4,5},{5,4},{6,7},{7,6},{8,9},{9,8},{10,11... | collective-permute-start | bytes 786440 | tf_op jit(solution)/shard_map/ppermute | solution.py:189
  126.0 14.4 %all_to_all.80 = bf16[8,64,256]{2,1,0:T(8,128)(2,1)S(1)} all-to-all(bf16[8,64,256]{2,1,0:T(8,128)(2,1)S(1)} %bitcast.34), channel_id=1, replica_groups=mesh['y'=4,'z'=8,'x'=4,'c'=2] {'z'}, dimensions={0} | all-to-all | bytes 524288 | tf_op jit(solution)/shard_map/all_to_all | solution.py:185
  140.5 18.7 %all_to_all.81 = f32[8,64,256]{2,1,0:T(8,128)S(1)} all-to-all(f32[8,64,256]{2,1,0:T(8,128)S(1)} %broadcast_in_dim.30), channel_id=1, replica_groups=mesh['y'=4,'z'=8,'x'=4,'c'=2] {'z'}, dimensions={0} | all-to-all | bytes 1048576 | tf_op jit(solution)/shard_map/all_to_all | solution.py:181
  159.1 2.2 collective-permute-start.7
  163.9 16.5 %all_to_all.82 = f32[16,48,256]{2,1,0:T(8,128)S(1)} all-to-all(f32[16,48,256]{2,1,0:T(8,128)S(1)} %products.9), channel_id=1, replica_groups=mesh['y'=4,'z'=8,'x'=4,'c'=2] {'x','y'}, dimensions={0} | all-to-all | bytes 1572864 | tf_op jit(solution)/shard_map/all_to_all | solution.py:185
  180.5 15.1 %all_to_all.83.s_ref = f32[16,48,256]{2,1,0:T(8,128)S(1)} all-to-all(f32[16,48,256]{2,1,0:T(8,128)S(1)} %broadcast_in_dim.31), channel_id=1, replica_groups=mesh['y'=4,'z'=8,'x'=4,'c'=2] {'x','y'}, dimensions={0} | all-to-all | bytes 1572864 | tf_op jit(solution)/shard_map/all_to_all | solution.py:181
  195.6 8.1 %factor_step.4 = bf16[512,256]{1,0:T(8,128)(2,1)S(1)} custom-call(f32[16,48,256]{2,1,0:T(8,128)S(1)} %all_to_all.83.s_ref), custom_call_target="tpu_custom_call" | custom-call | tf_op jit(solution)/shard_map/factor_step/pallas_call | solution.py:108
  204.0 3.5 %collective-permute-start.8 = (bf16[512,256]{1,0:T(8,128)(2,1)S(1)}, bf16[512,256]{1,0:T(8,128)(2,1)S(1)}, u32[]{:S(2)}, u32[]{:S(2)}) collective-permute-start(bf16[512,256]{1,0:T(8,128)(2,1)S(1)} %convolution_convert_fusion), channel_id=1, source_target_pairs={{0,1},{1,0},{2,3},{3,2},{4,5},{5,4},{6,7},{7,6},{8,9},{9,8},{10,11... | collective-permute-start | bytes 786440 | tf_op jit(solution)/shard_map/ppermute | solution.py:189
  209.0 14.7 %all_to_all.84 = bf16[8,64,256]{2,1,0:T(8,128)(2,1)S(1)} all-to-all(bf16[8,64,256]{2,1,0:T(8,128)(2,1)S(1)} %bitcast.35), channel_id=1, replica_groups=mesh['y'=4,'z'=8,'x'=4,'c'=2] {'z'}, dimensions={0} | all-to-all | bytes 524288 | tf_op jit(solution)/shard_map/all_to_all | solution.py:185
  223.8 19.8 %all_to_all.85 = f32[8,64,256]{2,1,0:T(8,128)S(1)} all-to-all(f32[8,64,256]{2,1,0:T(8,128)S(1)} %broadcast_in_dim.32), channel_id=1, replica_groups=mesh['y'=4,'z'=8,'x'=4,'c'=2] {'z'}, dimensions={0} | all-to-all | bytes 1048576 | tf_op jit(solution)/shard_map/all_to_all | solution.py:181
  247.2 16.5 %all_to_all.86 = f32[16,48,256]{2,1,0:T(8,128)S(1)} all-to-all(f32[16,48,256]{2,1,0:T(8,128)S(1)} %products.11), channel_id=1, replica_groups=mesh['y'=4,'z'=8,'x'=4,'c'=2] {'x','y'}, dimensions={0} | all-to-all | bytes 1572864 | tf_op jit(solution)/shard_map/all_to_all | solution.py:185
  264.7 3.8 %all-to-all-start.13 = ((f32[16,48,256]{2,1,0:T(8,128)}), f32[16,48,256]{2,1,0:T(8,128)S(1)}, u32[]{:S(2)}, u32[]{:S(2)}) async-start(f32[16,48,256]{2,1,0:T(8,128)} %broadcast_in_dim.33), calls=%async_computation.13 | async-start | bytes 1572864 | tf_op jit(solution)/shard_map/all_to_all | solution.py:181
  269.2 11.6 %all-to-all-done.13.s_ref = f32[16,48,256]{2,1,0:T(8,128)S(1)} async-done(((f32[16,48,256]{2,1,0:T(8,128)}), f32[16,48,256]{2,1,0:T(8,128)S(1)}, u32[]{:S(2)}, u32[]{:S(2)}) %all-to-all-start.13) | async-done | bytes 786464 | tf_op jit(solution)/shard_map/all_to_all | solution.py:181
  280.8 8.1 %factor_step.5 = (f32[512,256]{1,0:T(8,128)S(1)}, f32[256,256]{1,0:T(8,128)S(1)}) custom-call(f32[16,48,256]{2,1,0:T(8,128)S(1)} %all-to-all-done.13.s_ref), custom_call_target="tpu_custom_call" | custom-call | tf_op jit(solution)/shard_map/factor_step/pallas_call | solution.py:108
  289.0 2.8 collective-permute-start.10
  293.3 3.9 %collective-permute-start.11 = (f32[8,1024]{1,0:T(8,128)S(1)}, f32[8,1024]{1,0:T(8,128)S(1)}, u32[]{:S(2)}, u32[]{:S(2)}) collective-permute-start(f32[8,1024]{1,0:T(8,128)S(1)} %get-tuple-element.20), channel_id=1, source_target_pairs={{0,0},{1,128},{64,64},{65,192},{128,1},{129,129},{192,65},{193,193... | collective-permute-start | bytes 98312 | tf_op jit(solution)/shard_map/ppermute | solution.py:239
  297.9 3.3 %all-to-all-start.14 = ((f32[8,1,256]{2,1,0:T(1,128)}), f32[8,1,256]{2,1,0:T(1,128)S(1)}, u32[]{:S(2)}, u32[]{:S(2)}) async-start(f32[8,1,256]{2,1,0:T(1,128)} %broadcast_in_dim.35), calls=%async_computation.14 | async-start | bytes 16384 | tf_op jit(solution)/shard_map/all_to_all | solution.py:181
  301.3 6.4 %all-to-all-done.14.e_ref = f32[8,1,256]{2,1,0:T(1,128)S(1)} async-done(((f32[8,1,256]{2,1,0:T(1,128)}), f32[8,1,256]{2,1,0:T(1,128)S(1)}, u32[]{:S(2)}, u32[]{:S(2)}) %all-to-all-start.14) | async-done | bytes 8224 | tf_op jit(solution)/shard_map/all_to_all | solution.py:181
  307.7 1.6 finish.1
  (60 shorter events, 23.5 us)
Async XLA Ops:
  0.0 1.2 copy-start
  0.0 10.1 %copy-start.1 = (bf16[256,2048]{1,0:T(8,128)(2,1)S(1)}, bf16[256,2048]{1,0:T(8,128)(2,1)}, u32[]{:S(2)}) copy-start(bf16[256,2048]{1,0:T(8,128)(2,1)} %param.3) | copy-start | bytes 3145732
  3.6 13.0 %all-to-all-start = ((f32[8,32,256]{2,1,0:T(8,128)}), f32[8,32,256]{2,1,0:T(8,128)S(1)}, u32[]{:S(2)}, u32[]{:S(2)}) async-start(f32[8,32,256]{2,1,0:T(8,128)} %bitcast.2), calls=%async_computation | async-start | bytes 524288 | tf_op jit(solution)/shard_map/all_to_all | solution.py:185
  10.2 24.6 %collective-permute-start.1 = (bf16[256,1024]{1,0:T(8,128)(2,1)S(1)}, bf16[256,1024]{1,0:T(8,128)(2,1)S(1)}, u32[]{:S(2)}, u32[]{:S(2)}) collective-permute-start(bf16[256,1024]{1,0:T(8,128)(2,1)S(1)} %get-tuple-element.13), channel_id=1, source_target_pairs={{0,0},{1,128},{64,64},{65,192},{128,1},{129,129},{192,65},{193,193... | collective-permute-start | bytes 1572872 | tf_op jit(solution)/shard_map/ppermute | solution.py:198
  14.2 20.6 %collective-permute-start = (bf16[256,1024]{1,0:T(8,128)(2,1)S(1)}, bf16[256,1024]{1,0:T(8,128)(2,1)S(1)}, u32[]{:S(2)}, u32[]{:S(2)}) collective-permute-start(bf16[256,1024]{1,0:T(8,128)(2,1)S(1)} %get-tuple-element.14), channel_id=1, source_target_pairs={{0,64},{1,192},{64,0},{65,128},{128,65},{129,193},{192,1},{193,129... | collective-permute-start | bytes 1572872 | tf_op jit(solution)/shard_map/ppermute | solution.py:198
  25.3 8.1 %collective-permute-start.3 = (bf16[256,256]{1,0:T(8,128)(2,1)S(1)}, bf16[256,256]{1,0:T(8,128)(2,1)S(1)}, u32[]{:S(2)}, u32[]{:S(2)}) collective-permute-start(bf16[256,256]{1,0:T(8,128)(2,1)S(1)} %bitcast.36), channel_id=1, source_target_pairs={{0,0},{1,64},{64,128},{65,192},{128,1},{129,65},{192,129},{193,193... | collective-permute-start | bytes 393224 | tf_op jit(solution)/shard_map/ppermute | solution.py:207
  28.5 6.3 %collective-permute-start.2 = (bf16[256,256]{1,0:T(8,128)(2,1)S(1)}, bf16[256,256]{1,0:T(8,128)(2,1)S(1)}, u32[]{:S(2)}, u32[]{:S(2)}) collective-permute-start(bf16[256,256]{1,0:T(8,128)(2,1)S(1)} %bitcast.37), channel_id=1, source_target_pairs={{0,128},{1,192},{64,0},{65,64},{128,129},{129,193},{192,1},{193,65... | collective-permute-start | bytes 393224 | tf_op jit(solution)/shard_map/ppermute | solution.py:208
  35.4 1.6 collective-permute-start.4
  77.4 2.7 collective-permute-start.5
  121.0 4.6 %collective-permute-start.6 = (bf16[512,256]{1,0:T(8,128)(2,1)S(1)}, bf16[512,256]{1,0:T(8,128)(2,1)S(1)}, u32[]{:S(2)}, u32[]{:S(2)}) collective-permute-start(bf16[512,256]{1,0:T(8,128)(2,1)S(1)} %convolution_convert_fusion.1), channel_id=1, source_target_pairs={{0,1},{1,0},{2,3},{3,2},{4,5},{5,4},{6,7},{7,6},{8,9},{9,8},{10,11... | collective-permute-start | bytes 786440 | tf_op jit(solution)/shard_map/ppermute | solution.py:189
  159.1 3.7 %collective-permute-start.7 = (f32[512,256]{1,0:T(8,128)S(1)}, f32[512,256]{1,0:T(8,128)S(1)}, u32[]{:S(2)}, u32[]{:S(2)}) collective-permute-start(f32[512,256]{1,0:T(8,128)S(1)} %bitcast.31), channel_id=1, source_target_pairs={{0,1},{1,0},{2,3},{3,2},{4,5},{5,4},{6,7},{7,6},{8,9},{9,8},{10,11... | collective-permute-start | bytes 1572872 | tf_op jit(solution)/shard_map/ppermute | solution.py:189
  204.0 4.6 %collective-permute-start.8 = (bf16[512,256]{1,0:T(8,128)(2,1)S(1)}, bf16[512,256]{1,0:T(8,128)(2,1)S(1)}, u32[]{:S(2)}, u32[]{:S(2)}) collective-permute-start(bf16[512,256]{1,0:T(8,128)(2,1)S(1)} %convolution_convert_fusion), channel_id=1, source_target_pairs={{0,1},{1,0},{2,3},{3,2},{4,5},{5,4},{6,7},{7,6},{8,9},{9,8},{10,11... | collective-permute-start | bytes 786440 | tf_op jit(solution)/shard_map/ppermute | solution.py:189
  243.6 2.5 collective-permute-start.9
  264.7 16.1 %all-to-all-start.13 = ((f32[16,48,256]{2,1,0:T(8,128)}), f32[16,48,256]{2,1,0:T(8,128)S(1)}, u32[]{:S(2)}, u32[]{:S(2)}) async-start(f32[16,48,256]{2,1,0:T(8,128)} %broadcast_in_dim.33), calls=%async_computation.13 | async-start | bytes 1572864 | tf_op jit(solution)/shard_map/all_to_all | solution.py:181
  289.0 8.3 %collective-permute-start.10 = (f32[1,256]{1,0:T(1,128)S(1)}, f32[1,256]{1,0:T(1,128)S(1)}, u32[]{:S(2)}, u32[]{:S(2)}) collective-permute-start(f32[1,256]{1,0:T(1,128)S(1)} %bitcast.38), channel_id=1, source_target_pairs={{0,1},{1,0},{2,3},{3,2},{4,5},{5,4},{6,7},{7,6},{8,9},{9,8},{10,11... | collective-permute-start | bytes 3080 | tf_op jit(solution)/shard_map/ppermute | solution.py:189
  292.9 14.8 %collective-permute-start.12 = (f32[8,1024]{1,0:T(8,128)S(1)}, f32[8,1024]{1,0:T(8,128)S(1)}, u32[]{:S(2)}, u32[]{:S(2)}) collective-permute-start(f32[8,1024]{1,0:T(8,128)S(1)} %get-tuple-element.19), channel_id=1, source_target_pairs={{0,64},{1,192},{64,0},{65,128},{128,65},{129,193},{192,1},{193,129... | collective-permute-start | bytes 98312 | tf_op jit(solution)/shard_map/ppermute | solution.py:239
  293.3 14.4 %collective-permute-start.11 = (f32[8,1024]{1,0:T(8,128)S(1)}, f32[8,1024]{1,0:T(8,128)S(1)}, u32[]{:S(2)}, u32[]{:S(2)}) collective-permute-start(f32[8,1024]{1,0:T(8,128)S(1)} %get-tuple-element.20), channel_id=1, source_target_pairs={{0,0},{1,128},{64,64},{65,192},{128,1},{129,129},{192,65},{193,193... | collective-permute-start | bytes 98312 | tf_op jit(solution)/shard_map/ppermute | solution.py:239
  297.9 9.9 %all-to-all-start.14 = ((f32[8,1,256]{2,1,0:T(1,128)}), f32[8,1,256]{2,1,0:T(1,128)S(1)}, u32[]{:S(2)}, u32[]{:S(2)}) async-start(f32[8,1,256]{2,1,0:T(1,128)} %broadcast_in_dim.35), calls=%async_computation.14 | async-start | bytes 16384 | tf_op jit(solution)/shard_map/all_to_all | solution.py:181

commit v2 on v1

--- a/solution.py
+++ b/solution.py
@@ -92,19 +92,31 @@
 
 def step_kernel(s_ref, p_ref, x_ref, w_ref, b_ref, g_ref):
     for d in range(16):
-        g_ref[16 * d : 16 * d + 16, :] = s_ref[d, 0:16, :]
+        r = 8 * d
+        g_ref[r : r + 8, 0:LANES] = s_ref[d, 0:8, :]
+        g_ref[r : r + 8, LANES:L] = s_ref[d, 8:16, :]
+        g_ref[LANES + r : LANES + r + 8, LANES:L] = s_ref[d, 16:24, :]
     factor_inverse(g_ref, b_ref, w_ref, x_ref)
+    last = len(p_ref.shape) == 3
+    energy = jnp.zeros((1, L), f32)
     for n in range(2):
-        t = jnp.concatenate([s_ref[8 * n + d, 16:48, :] for d in range(8)], axis=0)
-        p_ref[256 * n : 256 * n + 256, :] = lax.dot_general(
-            t, x_ref[...], (((1,), (1,)), ((), ())), precision=HI, preferred_element_type=f32
-        ).astype(p_ref.dtype)
+        halves = [jnp.concatenate([s_ref[8 * n + d, h : h + 32, :] for d in range(8)], axis=0) for h in (24, 56)]
+        p = lax.dot_general(
+            jnp.concatenate(halves, axis=1), x_ref[...], (((1,), (1,)), ((), ())), precision=HI, preferred_element_type=f32
+        )
+        if last:
+            energy = energy + jnp.sum(p * p, axis=0, keepdims=True)
+        else:
+            p_ref[256 * n : 256 * n + 256, :] = p.astype(bf16)
+    if last:
+        for d in range(16):
+            p_ref[d] = energy
 
 
 def factor_step(s, last):
     shared = [vmem((LANES, 3 * LANES)), vmem((LANES, 3 * LANES)), vmem((L, L))]
     inverse = vmem((L, L))
-    projected = vmem((512, L), f32 if last else bf16)
+    projected = vmem((16, 1, L)) if last else vmem((512, L), bf16)
     return pl.pallas_call(
         step_kernel,
         out_shape=(projected, inverse) if last else projected,
@@ -123,20 +135,43 @@
     return a, b, (r - b.astype(f32)).astype(bf16)
 
 
+def whole_rows(i):
+    return jnp.concatenate([i[d] for d in range(8)], axis=0)
+
+
 def products_kernel(s_ref, i_ref, *refs):
     o_ref = refs[-1]
-    i = i_ref[...]
+    i = whole_rows(i_ref)
     t = sum(jnp.dot(s_ref[...], part, preferred_element_type=f32) for part in split(i))
-    g = tdot(i, i)
+    top = tdot(i[:, :LANES], i)
+    low = tdot(i[:, LANES:], i[:, LANES:])
     for d in range(16):
-        both = jnp.concatenate([g[16 * d : 16 * d + 16, :], t[32 * d : 32 * d + 32, :]], axis=0)
+        r, q = slice(8 * d, 8 * d + 8), slice(32 * d, 32 * d + 32)
+        both = jnp.concatenate([top[r, :LANES], top[r, LANES:], low[r, :], t[q, :LANES], t[q, LANES:]], axis=0)
         o_ref[d] = both if len(refs) == 1 else both + refs[0][d]
 
 
+def basis_kernel(r_ref, i_ref, o_ref):
+    o_ref[...] = lax.dot_general(
+        r_ref[...], whole_rows(i_ref), (((1,), (1,)), ((), ())), precision=HI, preferred_element_type=f32
+    )
+
+
+def basis_rows(rows, i):
+    return pl.pallas_call(
+        basis_kernel,
+        out_shape=vmem((16, 512)),
+        in_specs=[VMEM] * 2,
+        out_specs=VMEM,
+        compiler_params=limit(8),
+        name="basis_rows",
+    )(*near(rows, i))
+
+
 def products(s, i, *add):
     return pl.pallas_call(
         products_kernel,
-        out_shape=vmem((16, 48, L)),
+        out_shape=vmem((16, 88, LANES)),
         in_specs=[VMEM] * (2 + len(add)),
         out_specs=VMEM,
         compiler_params=limit(16),
@@ -146,7 +181,7 @@
 
 def finish_kernel(n_ref, e_ref, a_ref, b_ref, o_ref, t_ref):
     e = e_ref[0]
-    for d in range(1, 8):
+    for d in range(1, 16):
         e = e + e_ref[d]
     across = jnp.broadcast_to(e, (L, L))
     t_ref[...] = jnp.transpose(across)
@@ -214,24 +249,19 @@
 
         half = images(s_own) + swap(images(s_oth).astype(bf16)).astype(f32)
         chunk = scatter_sum(half.astype(bf16).reshape(8, 64, L), "z")
-        i_own = gather(chunk, "z", 8).reshape(512, L)
+        i_own = gather(chunk, "z", 8)
         i_oth = swap(i_own)
         both = products(s_oth, i_oth, products(s_own, i_own))
         sums = scatter_sum(both, ("x", "y"))
         whole = gather(sums, ("x", "y"), 16)
         if it < ITERS - 1:
             projected = factor_step(whole, False)
-    projected, inverse = factor_step(whole, True)
-    partial = jnp.sum(projected * projected, axis=0, keepdims=True)
-    partial = partial + swap(partial)
-    energies = gather(partial, "z", 8)
+    partial, inverse = factor_step(whole, True)
+    energies = lax.all_to_all(partial, ("z", "c"), 0, 0, tiled=True)
     rows = jnp.concatenate(
         [lax.dynamic_slice_in_dim(inverse, 8 * ((2 * c + (y + k) % 2) * 8 + z), 8, 0) for k in (0, 1)], axis=0
     )
-    own, oth = (
-        lax.dot_general(rows, i, (((1,), (1,)), ((), ())), precision=HI, preferred_element_type=f32)
-        for i in (i_own, i_oth)
-    )
+    own, oth = (basis_rows(rows, i) for i in (i_own, i_oth))
     basis = jnp.where(c == 0, jnp.concatenate([own, oth], axis=1), jnp.concatenate([oth, own], axis=1))
     out = []
     for k in (0, 1):

time: 310 us -> 303 us (0.977)
  waiting for transfers between devices: 29.3 us -> 25.2 us
    all_to_all x2 -> x1, waiting for transfers between devices: 18.1 us -> 11.1 us  [gather(): lax.all_to_all(jnp.broadcast_to(x, (n, *x.shape)), axis, 0, 0, tiled=True)]
    all_to_all x0 -> x1, starting transfers between devices: none -> 5.88 us  [body(): energies = lax.all_to_all(partial, ('z', 'c'), 0, 0, tiled=True)]
    ppermute x7 -> x6, starting transfers between devices: 14.2 us -> 9.46 us  [swap(): return lax.ppermute(x, 'c', [(0, 1), (1, 0)])]
    all_to_all x2 -> x1, starting transfers between devices: 7.17 us -> 3.85 us  [gather(): lax.all_to_all(jnp.broadcast_to(x, (n, *x.shape)), axis, 0, 0, tiled=True)]
    pallas_call x6 -> x8, Pallas kernels: 6.2 us -> 7.28 us  [the longest x6 6.23 us: products(): pl.pallas_call(products_kernel, out_shape=vmem((16, 88, LANES)), in_specs...]
  transfers between devices with their start and end apart: 16 -> 15, of which waited for: 11 -> 12; matrix products, arithmetic and copies ran while one was open for 1% -> 0% of each run, Pallas kernels for 1% -> 1%
where the time goes in v2:
time: 303 us; the launch traced here: 302 us
  blocking collectives  194 us (64%)
  starting transfers between devices  40 us (13%)
  Pallas kernels  33.7 us (11%)
  waiting for transfers between devices  25.2 us (8%)
  matrix products  4.44 us (1%)
    all_to_all x6, blocking collectives, gather(): lax.all_to_all(jnp.broadcast_to(x, (n, *x.shape)), axis, 0, 0, tiled=True)  97.9 us
    all_to_all x6, blocking collectives, scatter_sum(): lax.all_to_all(x, axis, 0, 0, tiled=True).astype(f32)  96.6 us
    pallas_call x3, Pallas kernels, factor_step(): pl.pallas_call(step_kernel, out_shape=(projected, inverse) if last else p...  24.8 us
    all_to_all x1, waiting for transfers between devices, gather(): lax.all_to_all(jnp.broadcast_to(x, (n, *x.shape)), axis, 0, 0, tiled=True)  11.1 us
    ppermute x6, starting transfers between devices, swap(): return lax.ppermute(x, 'c', [(0, 1), (1, 0)])  9.46 us
    all_to_all x1, starting transfers between devices, scatter_sum(): lax.all_to_all(x, axis, 0, 0, tiled=True).astype(f32)  6.51 us
    pallas_call x6, Pallas kernels, products(): pl.pallas_call(products_kernel, out_shape=vmem((16, 88, LANES)), in_specs...  6.23 us
  transfers between devices with their start and end apart: 15, of which 12 were waited for; matrix products, arithmetic and copies ran while one was open for 0% of the time, Pallas kernels for 1%

profile of v2, /device:TPU:1, one launch (start us, length us, event | category | flops | bytes accessed | tf_op | source)
XLA Modules:
  0.0 301.8 jit_solution(10985228576453970258)
XLA Ops:
  1.2 2.4 fusion.8
  3.6 6.5 %all-to-all-start = ((f32[8,32,256]{2,1,0:T(8,128)}), f32[8,32,256]{2,1,0:T(8,128)S(1)}, u32[]{:S(2)}, u32[]{:S(2)}) async-start(f32[8,32,256]{2,1,0:T(8,128)} %bitcast.2), calls=%async_computation | async-start | bytes 524288 | tf_op jit(solution)/shard_map/all_to_all | solution.py:220
  10.2 4.0 %collective-permute-start.1 = (bf16[256,1024]{1,0:T(8,128)(2,1)S(1)}, bf16[256,1024]{1,0:T(8,128)(2,1)S(1)}, u32[]{:S(2)}, u32[]{:S(2)}) collective-permute-start(bf16[256,1024]{1,0:T(8,128)(2,1)S(1)} %get-tuple-element.13), channel_id=1, source_target_pairs={{0,0},{1,128},{64,64},{65,192},{128,1},{129,129},{192,65},{193,193... | collective-permute-start | bytes 1572872 | tf_op jit(solution)/shard_map/ppermute | solution.py:233
  14.2 1.2 collective-permute-start
  16.6 8.7 %all_to_all.75 = bf16[8,32,256]{2,1,0:T(8,128)(2,1)S(1)} all-to-all(bf16[8,32,256]{2,1,0:T(8,128)(2,1)S(1)} %broadcast_in_dim.21), channel_id=1, replica_groups=mesh['y'=4,'z'=8,'x'=4,'c'=2] {'x','c'}, dimensions={0} | all-to-all | bytes 262144 | tf_op jit(solution)/shard_map/all_to_all | solution.py:216
  25.3 3.2 %collective-permute-start.3 = (bf16[256,256]{1,0:T(8,128)(2,1)S(1)}, bf16[256,256]{1,0:T(8,128)(2,1)S(1)}, u32[]{:S(2)}, u32[]{:S(2)}) collective-permute-start(bf16[256,256]{1,0:T(8,128)(2,1)S(1)} %bitcast.22), channel_id=1, source_target_pairs={{0,0},{1,64},{64,128},{65,192},{128,1},{129,65},{192,129},{193,193... | collective-permute-start | bytes 393224 | tf_op jit(solution)/shard_map/ppermute | solution.py:242
  28.5 1.5 collective-permute-start.2
  30.0 3.4 %collective-permute-done.3 = bf16[256,256]{1,0:T(8,128)(2,1)S(1)} collective-permute-done((bf16[256,256]{1,0:T(8,128)(2,1)S(1)}, bf16[256,256]{1,0:T(8,128)(2,1)S(1)}, u32[]{:S(2)}, u32[]{:S(2)}) %collective-permute-start.3) | collective-permute-done | bytes 131104 | tf_op jit(solution)/shard_map/ppermute | solution.py:242
  33.4 1.3 collective-permute-done.2
  35.6 1.5 collective-permute-done.4
  37.4 20.3 %all_to_all.76 = bf16[8,64,256]{2,1,0:T(8,128)(2,1)S(1)} all-to-all(bf16[8,64,256]{2,1,0:T(8,128)(2,1)S(1)} %bitcast.19), channel_id=1, replica_groups=mesh['y'=4,'z'=8,'x'=4,'c'=2] {'z'}, dimensions={0} | all-to-all | bytes 524288 | tf_op jit(solution)/shard_map/all_to_all | solution.py:220
  57.7 19.7 %all_to_all.77.i_ref = f32[8,64,256]{2,1,0:T(8,128)S(1)} all-to-all(f32[8,64,256]{2,1,0:T(8,128)S(1)} %broadcast_in_dim.22), channel_id=1, replica_groups=mesh['y'=4,'z'=8,'x'=4,'c'=2] {'z'}, dimensions={0} | all-to-all | bytes 1048576 | tf_op jit(solution)/shard_map/all_to_all | solution.py:216
  81.1 15.4 %all_to_all.78 = f32[16,88,128]{2,1,0:T(8,128)S(1)} all-to-all(f32[16,88,128]{2,1,0:T(8,128)S(1)} %products.7), channel_id=1, replica_groups=mesh['y'=4,'z'=8,'x'=4,'c'=2] {'x','y'}, dimensions={0} | all-to-all | bytes 1441792 | tf_op jit(solution)/shard_map/all_to_all | solution.py:220
  96.7 14.9 %all_to_all.79.s_ref = f32[16,88,128]{2,1,0:T(8,128)S(1)} all-to-all(f32[16,88,128]{2,1,0:T(8,128)S(1)} %broadcast_in_dim.23), channel_id=1, replica_groups=mesh['y'=4,'z'=8,'x'=4,'c'=2] {'x','y'}, dimensions={0} | all-to-all | bytes 1441792 | tf_op jit(solution)/shard_map/all_to_all | solution.py:216
  111.6 8.1 %factor_step.3 = bf16[512,256]{1,0:T(8,128)(2,1)S(1)} custom-call(f32[16,88,128]{2,1,0:T(8,128)S(1)} %all_to_all.79.s_ref), custom_call_target="tpu_custom_call" | custom-call | tf_op jit(solution)/shard_map/factor_step/pallas_call | solution.py:120
  120.0 3.1 %collective-permute-start.6 = (bf16[512,256]{1,0:T(8,128)(2,1)S(1)}, bf16[512,256]{1,0:T(8,128)(2,1)S(1)}, u32[]{:S(2)}, u32[]{:S(2)}) collective-permute-start(bf16[512,256]{1,0:T(8,128)(2,1)S(1)} %convolution_convert_fusion.1), channel_id=1, source_target_pairs={{0,1},{1,0},{2,3},{3,2},{4,5},{5,4},{6,7},{7,6},{8,9},{9,8},{10,11... | collective-permute-start | bytes 786440 | tf_op jit(solution)/shard_map/ppermute | solution.py:224
  124.6 14.9 %all_to_all.80 = bf16[8,64,256]{2,1,0:T(8,128)(2,1)S(1)} all-to-all(bf16[8,64,256]{2,1,0:T(8,128)(2,1)S(1)} %bitcast.20), channel_id=1, replica_groups=mesh['y'=4,'z'=8,'x'=4,'c'=2] {'z'}, dimensions={0} | all-to-all | bytes 524288 | tf_op jit(solution)/shard_map/all_to_all | solution.py:220
  139.6 19.8 %all_to_all.81.i_ref = f32[8,64,256]{2,1,0:T(8,128)S(1)} all-to-all(f32[8,64,256]{2,1,0:T(8,128)S(1)} %broadcast_in_dim.24), channel_id=1, replica_groups=mesh['y'=4,'z'=8,'x'=4,'c'=2] {'z'}, dimensions={0} | all-to-all | bytes 1048576 | tf_op jit(solution)/shard_map/all_to_all | solution.py:216
  163.0 15.7 %all_to_all.82 = f32[16,88,128]{2,1,0:T(8,128)S(1)} all-to-all(f32[16,88,128]{2,1,0:T(8,128)S(1)} %products.9), channel_id=1, replica_groups=mesh['y'=4,'z'=8,'x'=4,'c'=2] {'x','y'}, dimensions={0} | all-to-all | bytes 1441792 | tf_op jit(solution)/shard_map/all_to_all | solution.py:220
  178.8 14.9 %all_to_all.83.s_ref = f32[16,88,128]{2,1,0:T(8,128)S(1)} all-to-all(f32[16,88,128]{2,1,0:T(8,128)S(1)} %broadcast_in_dim.25), channel_id=1, replica_groups=mesh['y'=4,'z'=8,'x'=4,'c'=2] {'x','y'}, dimensions={0} | all-to-all | bytes 1441792 | tf_op jit(solution)/shard_map/all_to_all | solution.py:216
  193.7 8.1 %factor_step.4 = bf16[512,256]{1,0:T(8,128)(2,1)S(1)} custom-call(f32[16,88,128]{2,1,0:T(8,128)S(1)} %all_to_all.83.s_ref), custom_call_target="tpu_custom_call" | custom-call | tf_op jit(solution)/shard_map/factor_step/pallas_call | solution.py:120
  202.1 3.1 %collective-permute-start.8 = (bf16[512,256]{1,0:T(8,128)(2,1)S(1)}, bf16[512,256]{1,0:T(8,128)(2,1)S(1)}, u32[]{:S(2)}, u32[]{:S(2)}) collective-permute-start(bf16[512,256]{1,0:T(8,128)(2,1)S(1)} %convolution_convert_fusion), channel_id=1, source_target_pairs={{0,1},{1,0},{2,3},{3,2},{4,5},{5,4},{6,7},{7,6},{8,9},{9,8},{10,11... | collective-permute-start | bytes 786440 | tf_op jit(solution)/shard_map/ppermute | solution.py:224
  206.7 14.7 %all_to_all.84 = bf16[8,64,256]{2,1,0:T(8,128)(2,1)S(1)} all-to-all(bf16[8,64,256]{2,1,0:T(8,128)(2,1)S(1)} %bitcast.21), channel_id=1, replica_groups=mesh['y'=4,'z'=8,'x'=4,'c'=2] {'z'}, dimensions={0} | all-to-all | bytes 524288 | tf_op jit(solution)/shard_map/all_to_all | solution.py:220
  221.5 19.8 %all_to_all.85.i_ref = f32[8,64,256]{2,1,0:T(8,128)S(1)} all-to-all(f32[8,64,256]{2,1,0:T(8,128)S(1)} %broadcast_in_dim.26), channel_id=1, replica_groups=mesh['y'=4,'z'=8,'x'=4,'c'=2] {'z'}, dimensions={0} | all-to-all | bytes 1048576 | tf_op jit(solution)/shard_map/all_to_all | solution.py:216
  244.9 15.6 %all_to_all.86 = f32[16,88,128]{2,1,0:T(8,128)S(1)} all-to-all(f32[16,88,128]{2,1,0:T(8,128)S(1)} %products.11), channel_id=1, replica_groups=mesh['y'=4,'z'=8,'x'=4,'c'=2] {'x','y'}, dimensions={0} | all-to-all | bytes 1441792 | tf_op jit(solution)/shard_map/all_to_all | solution.py:220
  261.5 3.8 %all-to-all-start.13 = ((f32[16,88,128]{2,1,0:T(8,128)}), f32[16,88,128]{2,1,0:T(8,128)S(1)}, u32[]{:S(2)}, u32[]{:S(2)}) async-start(f32[16,88,128]{2,1,0:T(8,128)} %broadcast_in_dim.27), calls=%async_computation.13 | async-start | bytes 1441792 | tf_op jit(solution)/shard_map/all_to_all | solution.py:216
  266.1 11.1 %all-to-all-done.13.s_ref = f32[16,88,128]{2,1,0:T(8,128)S(1)} async-done(((f32[16,88,128]{2,1,0:T(8,128)}), f32[16,88,128]{2,1,0:T(8,128)S(1)}, u32[]{:S(2)}, u32[]{:S(2)}) %all-to-all-start.13) | async-done | bytes 720928 | tf_op jit(solution)/shard_map/all_to_all | solution.py:216
  277.2 8.7 %factor_step.5 = (f32[16,1,256]{2,1,0:T(1,128)}, f32[256,256]{1,0:T(8,128)S(1)}) custom-call(f32[16,88,128]{2,1,0:T(8,128)S(1)} %all-to-all-done.13.s_ref), custom_call_target="tpu_custom_call" | custom-call | tf_op jit(solution)/shard_map/factor_step/pallas_call | solution.py:120
  285.9 5.9 %all-to-all-start.14 = ((f32[16,1,256]{2,1,0:T(1,128)}), f32[16,1,256]{2,1,0:T(1,128)S(1)}, u32[]{:S(2)}, u32[]{:S(2)}) async-start(f32[16,1,256]{2,1,0:T(1,128)} %get-tuple-element.7), calls=%async_computation.14 | async-start | bytes 32768 | tf_op jit(solution)/shard_map/all_to_all | solution.py:260
  293.5 3.8 %collective-permute-start.10 = (f32[8,1024]{1,0:T(8,128)S(1)}, f32[8,1024]{1,0:T(8,128)S(1)}, u32[]{:S(2)}, u32[]{:S(2)}) collective-permute-start(f32[8,1024]{1,0:T(8,128)S(1)} %get-tuple-element.20), channel_id=1, source_target_pairs={{0,0},{1,128},{64,64},{65,192},{128,1},{129,129},{192,65},{193,193... | collective-permute-start | bytes 98312 | tf_op jit(solution)/shard_map/ppermute | solution.py:269
  297.3 1.8 all-to-all-done.14.e_ref
  300.2 1.6 finish.1
  (56 shorter events, 22.3 us)
Async XLA Ops:
  0.0 1.2 copy-start
  0.0 10.1 %copy-start.1 = (bf16[256,2048]{1,0:T(8,128)(2,1)S(1)}, bf16[256,2048]{1,0:T(8,128)(2,1)}, u32[]{:S(2)}) copy-start(bf16[256,2048]{1,0:T(8,128)(2,1)} %param.3) | copy-start | bytes 3145732
  3.6 13.0 %all-to-all-start = ((f32[8,32,256]{2,1,0:T(8,128)}), f32[8,32,256]{2,1,0:T(8,128)S(1)}, u32[]{:S(2)}, u32[]{:S(2)}) async-start(f32[8,32,256]{2,1,0:T(8,128)} %bitcast.2), calls=%async_computation | async-start | bytes 524288 | tf_op jit(solution)/shard_map/all_to_all | solution.py:220
  10.2 24.6 %collective-permute-start.1 = (bf16[256,1024]{1,0:T(8,128)(2,1)S(1)}, bf16[256,1024]{1,0:T(8,128)(2,1)S(1)}, u32[]{:S(2)}, u32[]{:S(2)}) collective-permute-start(bf16[256,1024]{1,0:T(8,128)(2,1)S(1)} %get-tuple-element.13), channel_id=1, source_target_pairs={{0,0},{1,128},{64,64},{65,192},{128,1},{129,129},{192,65},{193,193... | collective-permute-start | bytes 1572872 | tf_op jit(solution)/shard_map/ppermute | solution.py:233
  14.2 20.6 %collective-permute-start = (bf16[256,1024]{1,0:T(8,128)(2,1)S(1)}, bf16[256,1024]{1,0:T(8,128)(2,1)S(1)}, u32[]{:S(2)}, u32[]{:S(2)}) collective-permute-start(bf16[256,1024]{1,0:T(8,128)(2,1)S(1)} %get-tuple-element.14), channel_id=1, source_target_pairs={{0,64},{1,192},{64,0},{65,128},{128,65},{129,193},{192,1},{193,129... | collective-permute-start | bytes 1572872 | tf_op jit(solution)/shard_map/ppermute | solution.py:233
  25.3 8.1 %collective-permute-start.3 = (bf16[256,256]{1,0:T(8,128)(2,1)S(1)}, bf16[256,256]{1,0:T(8,128)(2,1)S(1)}, u32[]{:S(2)}, u32[]{:S(2)}) collective-permute-start(bf16[256,256]{1,0:T(8,128)(2,1)S(1)} %bitcast.22), channel_id=1, source_target_pairs={{0,0},{1,64},{64,128},{65,192},{128,1},{129,65},{192,129},{193,193... | collective-permute-start | bytes 393224 | tf_op jit(solution)/shard_map/ppermute | solution.py:242
  28.5 6.3 %collective-permute-start.2 = (bf16[256,256]{1,0:T(8,128)(2,1)S(1)}, bf16[256,256]{1,0:T(8,128)(2,1)S(1)}, u32[]{:S(2)}, u32[]{:S(2)}) collective-permute-start(bf16[256,256]{1,0:T(8,128)(2,1)S(1)} %bitcast.23), channel_id=1, source_target_pairs={{0,128},{1,192},{64,0},{65,64},{128,129},{129,193},{192,1},{193,65... | collective-permute-start | bytes 393224 | tf_op jit(solution)/shard_map/ppermute | solution.py:243
  35.4 1.6 collective-permute-start.4
  77.4 2.7 collective-permute-start.5
  120.0 4.2 %collective-permute-start.6 = (bf16[512,256]{1,0:T(8,128)(2,1)S(1)}, bf16[512,256]{1,0:T(8,128)(2,1)S(1)}, u32[]{:S(2)}, u32[]{:S(2)}) collective-permute-start(bf16[512,256]{1,0:T(8,128)(2,1)S(1)} %convolution_convert_fusion.1), channel_id=1, source_target_pairs={{0,1},{1,0},{2,3},{3,2},{4,5},{5,4},{6,7},{7,6},{8,9},{9,8},{10,11... | collective-permute-start | bytes 786440 | tf_op jit(solution)/shard_map/ppermute | solution.py:224
  159.4 2.5 collective-permute-start.7
  202.1 4.2 %collective-permute-start.8 = (bf16[512,256]{1,0:T(8,128)(2,1)S(1)}, bf16[512,256]{1,0:T(8,128)(2,1)S(1)}, u32[]{:S(2)}, u32[]{:S(2)}) collective-permute-start(bf16[512,256]{1,0:T(8,128)(2,1)S(1)} %convolution_convert_fusion), channel_id=1, source_target_pairs={{0,1},{1,0},{2,3},{3,2},{4,5},{5,4},{6,7},{7,6},{8,9},{9,8},{10,11... | collective-permute-start | bytes 786440 | tf_op jit(solution)/shard_map/ppermute | solution.py:224
  241.3 2.5 collective-permute-start.9
  261.5 15.7 %all-to-all-start.13 = ((f32[16,88,128]{2,1,0:T(8,128)}), f32[16,88,128]{2,1,0:T(8,128)S(1)}, u32[]{:S(2)}, u32[]{:S(2)}) async-start(f32[16,88,128]{2,1,0:T(8,128)} %broadcast_in_dim.27), calls=%async_computation.13 | async-start | bytes 1441792 | tf_op jit(solution)/shard_map/all_to_all | solution.py:216
  285.9 13.3 %all-to-all-start.14 = ((f32[16,1,256]{2,1,0:T(1,128)}), f32[16,1,256]{2,1,0:T(1,128)S(1)}, u32[]{:S(2)}, u32[]{:S(2)}) async-start(f32[16,1,256]{2,1,0:T(1,128)} %get-tuple-element.7), calls=%async_computation.14 | async-start | bytes 32768 | tf_op jit(solution)/shard_map/all_to_all | solution.py:260
  292.9 6.3 %collective-permute-start.11 = (f32[8,1024]{1,0:T(8,128)S(1)}, f32[8,1024]{1,0:T(8,128)S(1)}, u32[]{:S(2)}, u32[]{:S(2)}) collective-permute-start(f32[8,1024]{1,0:T(8,128)S(1)} %get-tuple-element.19), channel_id=1, source_target_pairs={{0,64},{1,192},{64,0},{65,128},{128,65},{129,193},{192,1},{193,129... | collective-permute-start | bytes 98312 | tf_op jit(solution)/shard_map/ppermute | solution.py:269
  293.5 6.7 %collective-permute-start.10 = (f32[8,1024]{1,0:T(8,128)S(1)}, f32[8,1024]{1,0:T(8,128)S(1)}, u32[]{:S(2)}, u32[]{:S(2)}) collective-permute-start(f32[8,1024]{1,0:T(8,128)S(1)} %get-tuple-element.20), channel_id=1, source_target_pairs={{0,0},{1,128},{64,64},{65,192},{128,1},{129,129},{192,65},{193,193... | collective-permute-start | bytes 98312 | tf_op jit(solution)/shard_map/ppermute | solution.py:269

commit v3 on v2

--- a/solution.py
+++ b/solution.py
@@ -247,7 +247,8 @@
         def images(part):
             return lax.dot_general(part, projected, (((0,), (0,)), ((), ())), preferred_element_type=f32)
 
-        half = images(s_own) + swap(images(s_oth).astype(bf16)).astype(f32)
+        sent = swap(images(s_oth).astype(bf16))
+        half = lax.optimization_barrier(images(s_own)) + sent.astype(f32)
         chunk = scatter_sum(half.astype(bf16).reshape(8, 64, L), "z")
         i_own = gather(chunk, "z", 8)
         i_oth = swap(i_own)

time: 303 us -> 302 us (level)
  no operation moved by 1% of the time
where the time goes in v3:
time: 302 us; the launch traced here: 301 us
  blocking collectives  194 us (64%)
  starting transfers between devices  40.5 us (13%)
  Pallas kernels  33.7 us (11%)
  waiting for transfers between devices  23.8 us (8%)
  matrix products  4.41 us (1%)
    all_to_all x6, blocking collectives, gather(): lax.all_to_all(jnp.broadcast_to(x, (n, *x.shape)), axis, 0, 0, tiled=True)  97.9 us
    all_to_all x6, blocking collectives, scatter_sum(): lax.all_to_all(x, axis, 0, 0, tiled=True).astype(f32)  96.4 us
    pallas_call x3, Pallas kernels, factor_step(): pl.pallas_call(step_kernel, out_shape=(projected, inverse) if last else p...  24.8 us
    all_to_all x1, waiting for transfers between devices, gather(): lax.all_to_all(jnp.broadcast_to(x, (n, *x.shape)), axis, 0, 0, tiled=True)  10.8 us
    ppermute x6, starting transfers between devices, swap(): return lax.ppermute(x, 'c', [(0, 1), (1, 0)])  9.64 us
    all_to_all x1, starting transfers between devices, scatter_sum(): lax.all_to_all(x, axis, 0, 0, tiled=True).astype(f32)  6.51 us
    all_to_all x1, starting transfers between devices, body(): energies = lax.all_to_all(partial, ('z', 'c'), 0, 0, tiled=True)  6.26 us
    pallas_call x6, Pallas kernels, products(): pl.pallas_call(products_kernel, out_shape=vmem((16, 88, LANES)), in_specs...  6.23 us
  transfers between devices with their start and end apart: 15, of which 12 were waited for; matrix products, arithmetic and copies ran while one was open for 0% of the time, Pallas kernels for 1%

profile of v3, /device:TPU:1, one launch (start us, length us, event | category | flops | bytes accessed | tf_op | source)
XLA Modules:
  0.0 300.9 jit_solution(4206224293184684157)
XLA Ops:
  0.0 1.2 copy-done
  1.2 2.4 fusion.6
  3.6 6.5 %all-to-all-start = ((f32[8,32,256]{2,1,0:T(8,128)}), f32[8,32,256]{2,1,0:T(8,128)S(1)}, u32[]{:S(2)}, u32[]{:S(2)}) async-start(f32[8,32,256]{2,1,0:T(8,128)} %bitcast.2), calls=%async_computation | async-start | bytes 524288 | tf_op jit(solution)/shard_map/all_to_all | solution.py:220
  10.2 4.0 %collective-permute-start.1 = (bf16[256,1024]{1,0:T(8,128)(2,1)S(1)}, bf16[256,1024]{1,0:T(8,128)(2,1)S(1)}, u32[]{:S(2)}, u32[]{:S(2)}) collective-permute-start(bf16[256,1024]{1,0:T(8,128)(2,1)S(1)} %get-tuple-element.13), channel_id=1, source_target_pairs={{0,0},{1,128},{64,64},{65,192},{128,1},{129,129},{192,65},{193,193... | collective-permute-start | bytes 1572872 | tf_op jit(solution)/shard_map/ppermute | solution.py:233
  14.2 1.2 collective-permute-start
  16.6 8.7 %all_to_all.75 = bf16[8,32,256]{2,1,0:T(8,128)(2,1)S(1)} all-to-all(bf16[8,32,256]{2,1,0:T(8,128)(2,1)S(1)} %broadcast_in_dim.21), channel_id=1, replica_groups=mesh['y'=4,'z'=8,'x'=4,'c'=2] {'x','c'}, dimensions={0} | all-to-all | bytes 262144 | tf_op jit(solution)/shard_map/all_to_all | solution.py:216
  25.3 3.2 %collective-permute-start.3 = (bf16[256,256]{1,0:T(8,128)(2,1)S(1)}, bf16[256,256]{1,0:T(8,128)(2,1)S(1)}, u32[]{:S(2)}, u32[]{:S(2)}) collective-permute-start(bf16[256,256]{1,0:T(8,128)(2,1)S(1)} %bitcast.22), channel_id=1, source_target_pairs={{0,0},{1,64},{64,128},{65,192},{128,1},{129,65},{192,129},{193,193... | collective-permute-start | bytes 393224 | tf_op jit(solution)/shard_map/ppermute | solution.py:242
  28.5 1.5 collective-permute-start.2
  30.0 3.4 %collective-permute-done.3 = bf16[256,256]{1,0:T(8,128)(2,1)S(1)} collective-permute-done((bf16[256,256]{1,0:T(8,128)(2,1)S(1)}, bf16[256,256]{1,0:T(8,128)(2,1)S(1)}, u32[]{:S(2)}, u32[]{:S(2)}) %collective-permute-start.3) | collective-permute-done | bytes 131104 | tf_op jit(solution)/shard_map/ppermute | solution.py:242
  33.4 1.3 collective-permute-done.2
  37.1 20.3 %all_to_all.76 = bf16[8,64,256]{2,1,0:T(8,128)(2,1)S(1)} all-to-all(bf16[8,64,256]{2,1,0:T(8,128)(2,1)S(1)} %bitcast.19), channel_id=1, replica_groups=mesh['y'=4,'z'=8,'x'=4,'c'=2] {'z'}, dimensions={0} | all-to-all | bytes 524288 | tf_op jit(solution)/shard_map/all_to_all | solution.py:220
  57.4 19.7 %all_to_all.77.i_ref = f32[8,64,256]{2,1,0:T(8,128)S(1)} all-to-all(f32[8,64,256]{2,1,0:T(8,128)S(1)} %broadcast_in_dim.22), channel_id=1, replica_groups=mesh['y'=4,'z'=8,'x'=4,'c'=2] {'z'}, dimensions={0} | all-to-all | bytes 1048576 | tf_op jit(solution)/shard_map/all_to_all | solution.py:216
  80.9 15.4 %all_to_all.78 = f32[16,88,128]{2,1,0:T(8,128)S(1)} all-to-all(f32[16,88,128]{2,1,0:T(8,128)S(1)} %products.7), channel_id=1, replica_groups=mesh['y'=4,'z'=8,'x'=4,'c'=2] {'x','y'}, dimensions={0} | all-to-all | bytes 1441792 | tf_op jit(solution)/shard_map/all_to_all | solution.py:220
  96.4 14.9 %all_to_all.79.s_ref = f32[16,88,128]{2,1,0:T(8,128)S(1)} all-to-all(f32[16,88,128]{2,1,0:T(8,128)S(1)} %broadcast_in_dim.23), channel_id=1, replica_groups=mesh['y'=4,'z'=8,'x'=4,'c'=2] {'x','y'}, dimensions={0} | all-to-all | bytes 1441792 | tf_op jit(solution)/shard_map/all_to_all | solution.py:216
  111.3 8.1 %factor_step.3 = bf16[512,256]{1,0:T(8,128)(2,1)S(1)} custom-call(f32[16,88,128]{2,1,0:T(8,128)S(1)} %all_to_all.79.s_ref), custom_call_target="tpu_custom_call" | custom-call | tf_op jit(solution)/shard_map/factor_step/pallas_call | solution.py:120
  119.7 3.3 %collective-permute-start.6 = (bf16[512,256]{1,0:T(8,128)(2,1)S(1)}, bf16[512,256]{1,0:T(8,128)(2,1)S(1)}, u32[]{:S(2)}, u32[]{:S(2)}) collective-permute-start(bf16[512,256]{1,0:T(8,128)(2,1)S(1)} %convolution_convert_fusion.1), channel_id=1, source_target_pairs={{0,1},{1,0},{2,3},{3,2},{4,5},{5,4},{6,7},{7,6},{8,9},{9,8},{10,11... | collective-permute-start | bytes 786440 | tf_op jit(solution)/shard_map/ppermute | solution.py:224
  124.2 14.7 %all_to_all.80 = bf16[8,64,256]{2,1,0:T(8,128)(2,1)S(1)} all-to-all(bf16[8,64,256]{2,1,0:T(8,128)(2,1)S(1)} %bitcast.20), channel_id=1, replica_groups=mesh['y'=4,'z'=8,'x'=4,'c'=2] {'z'}, dimensions={0} | all-to-all | bytes 524288 | tf_op jit(solution)/shard_map/all_to_all | solution.py:220
  139.0 19.8 %all_to_all.81.i_ref = f32[8,64,256]{2,1,0:T(8,128)S(1)} all-to-all(f32[8,64,256]{2,1,0:T(8,128)S(1)} %broadcast_in_dim.24), channel_id=1, replica_groups=mesh['y'=4,'z'=8,'x'=4,'c'=2] {'z'}, dimensions={0} | all-to-all | bytes 1048576 | tf_op jit(solution)/shard_map/all_to_all | solution.py:216
  162.4 15.6 %all_to_all.82 = f32[16,88,128]{2,1,0:T(8,128)S(1)} all-to-all(f32[16,88,128]{2,1,0:T(8,128)S(1)} %products.9), channel_id=1, replica_groups=mesh['y'=4,'z'=8,'x'=4,'c'=2] {'x','y'}, dimensions={0} | all-to-all | bytes 1441792 | tf_op jit(solution)/shard_map/all_to_all | solution.py:220
  178.2 14.9 %all_to_all.83.s_ref = f32[16,88,128]{2,1,0:T(8,128)S(1)} all-to-all(f32[16,88,128]{2,1,0:T(8,128)S(1)} %broadcast_in_dim.25), channel_id=1, replica_groups=mesh['y'=4,'z'=8,'x'=4,'c'=2] {'x','y'}, dimensions={0} | all-to-all | bytes 1441792 | tf_op jit(solution)/shard_map/all_to_all | solution.py:216
  193.1 8.1 %factor_step.4 = bf16[512,256]{1,0:T(8,128)(2,1)S(1)} custom-call(f32[16,88,128]{2,1,0:T(8,128)S(1)} %all_to_all.83.s_ref), custom_call_target="tpu_custom_call" | custom-call | tf_op jit(solution)/shard_map/factor_step/pallas_call | solution.py:120
  201.5 3.1 %collective-permute-start.8 = (bf16[512,256]{1,0:T(8,128)(2,1)S(1)}, bf16[512,256]{1,0:T(8,128)(2,1)S(1)}, u32[]{:S(2)}, u32[]{:S(2)}) collective-permute-start(bf16[512,256]{1,0:T(8,128)(2,1)S(1)} %convolution_convert_fusion), channel_id=1, source_target_pairs={{0,1},{1,0},{2,3},{3,2},{4,5},{5,4},{6,7},{7,6},{8,9},{9,8},{10,11... | collective-permute-start | bytes 786440 | tf_op jit(solution)/shard_map/ppermute | solution.py:224
  205.8 14.7 %all_to_all.84 = bf16[8,64,256]{2,1,0:T(8,128)(2,1)S(1)} all-to-all(bf16[8,64,256]{2,1,0:T(8,128)(2,1)S(1)} %bitcast.21), channel_id=1, replica_groups=mesh['y'=4,'z'=8,'x'=4,'c'=2] {'z'}, dimensions={0} | all-to-all | bytes 524288 | tf_op jit(solution)/shard_map/all_to_all | solution.py:220
  220.6 19.8 %all_to_all.85.i_ref = f32[8,64,256]{2,1,0:T(8,128)S(1)} all-to-all(f32[8,64,256]{2,1,0:T(8,128)S(1)} %broadcast_in_dim.26), channel_id=1, replica_groups=mesh['y'=4,'z'=8,'x'=4,'c'=2] {'z'}, dimensions={0} | all-to-all | bytes 1048576 | tf_op jit(solution)/shard_map/all_to_all | solution.py:216
  244.0 15.6 %all_to_all.86 = f32[16,88,128]{2,1,0:T(8,128)S(1)} all-to-all(f32[16,88,128]{2,1,0:T(8,128)S(1)} %products.11), channel_id=1, replica_groups=mesh['y'=4,'z'=8,'x'=4,'c'=2] {'x','y'}, dimensions={0} | all-to-all | bytes 1441792 | tf_op jit(solution)/shard_map/all_to_all | solution.py:220
  260.7 3.8 %all-to-all-start.13 = ((f32[16,88,128]{2,1,0:T(8,128)}), f32[16,88,128]{2,1,0:T(8,128)S(1)}, u32[]{:S(2)}, u32[]{:S(2)}) async-start(f32[16,88,128]{2,1,0:T(8,128)} %broadcast_in_dim.27), calls=%async_computation.13 | async-start | bytes 1441792 | tf_op jit(solution)/shard_map/all_to_all | solution.py:216
  265.2 10.8 %all-to-all-done.13.s_ref = f32[16,88,128]{2,1,0:T(8,128)S(1)} async-done(((f32[16,88,128]{2,1,0:T(8,128)}), f32[16,88,128]{2,1,0:T(8,128)S(1)}, u32[]{:S(2)}, u32[]{:S(2)}) %all-to-all-start.13) | async-done | bytes 720928 | tf_op jit(solution)/shard_map/all_to_all | solution.py:216
  276.0 8.7 %factor_step.5 = (f32[16,1,256]{2,1,0:T(1,128)}, f32[256,256]{1,0:T(8,128)S(1)}) custom-call(f32[16,88,128]{2,1,0:T(8,128)S(1)} %all-to-all-done.13.s_ref), custom_call_target="tpu_custom_call" | custom-call | tf_op jit(solution)/shard_map/factor_step/pallas_call | solution.py:120
  284.7 6.3 %all-to-all-start.14 = ((f32[16,1,256]{2,1,0:T(1,128)}), f32[16,1,256]{2,1,0:T(1,128)S(1)}, u32[]{:S(2)}, u32[]{:S(2)}) async-start(f32[16,1,256]{2,1,0:T(1,128)} %get-tuple-element.7), calls=%async_computation.14 | async-start | bytes 32768 | tf_op jit(solution)/shard_map/all_to_all | solution.py:261
  292.6 3.8 %collective-permute-start.10 = (f32[8,1024]{1,0:T(8,128)S(1)}, f32[8,1024]{1,0:T(8,128)S(1)}, u32[]{:S(2)}, u32[]{:S(2)}) collective-permute-start(f32[8,1024]{1,0:T(8,128)S(1)} %get-tuple-element.20), channel_id=1, source_target_pairs={{0,0},{1,128},{64,64},{65,192},{128,1},{129,129},{192,65},{193,193... | collective-permute-start | bytes 98312 | tf_op jit(solution)/shard_map/ppermute | solution.py:270
  296.5 1.8 all-to-all-done.14.e_ref
  299.3 1.6 finish.1
  (59 shorter events, 21.5 us)
Async XLA Ops:
  0.0 1.2 copy-start
  0.0 10.1 %copy-start.1 = (bf16[256,2048]{1,0:T(8,128)(2,1)S(1)}, bf16[256,2048]{1,0:T(8,128)(2,1)}, u32[]{:S(2)}) copy-start(bf16[256,2048]{1,0:T(8,128)(2,1)} %param.3) | copy-start | bytes 3145732
  3.6 13.0 %all-to-all-start = ((f32[8,32,256]{2,1,0:T(8,128)}), f32[8,32,256]{2,1,0:T(8,128)S(1)}, u32[]{:S(2)}, u32[]{:S(2)}) async-start(f32[8,32,256]{2,1,0:T(8,128)} %bitcast.2), calls=%async_computation | async-start | bytes 524288 | tf_op jit(solution)/shard_map/all_to_all | solution.py:220
  10.2 24.6 %collective-permute-start.1 = (bf16[256,1024]{1,0:T(8,128)(2,1)S(1)}, bf16[256,1024]{1,0:T(8,128)(2,1)S(1)}, u32[]{:S(2)}, u32[]{:S(2)}) collective-permute-start(bf16[256,1024]{1,0:T(8,128)(2,1)S(1)} %get-tuple-element.13), channel_id=1, source_target_pairs={{0,0},{1,128},{64,64},{65,192},{128,1},{129,129},{192,65},{193,193... | collective-permute-start | bytes 1572872 | tf_op jit(solution)/shard_map/ppermute | solution.py:233
  14.2 20.6 %collective-permute-start = (bf16[256,1024]{1,0:T(8,128)(2,1)S(1)}, bf16[256,1024]{1,0:T(8,128)(2,1)S(1)}, u32[]{:S(2)}, u32[]{:S(2)}) collective-permute-start(bf16[256,1024]{1,0:T(8,128)(2,1)S(1)} %get-tuple-element.14), channel_id=1, source_target_pairs={{0,64},{1,192},{64,0},{65,128},{128,65},{129,193},{192,1},{193,129... | collective-permute-start | bytes 1572872 | tf_op jit(solution)/shard_map/ppermute | solution.py:233
  25.3 8.1 %collective-permute-start.3 = (bf16[256,256]{1,0:T(8,128)(2,1)S(1)}, bf16[256,256]{1,0:T(8,128)(2,1)S(1)}, u32[]{:S(2)}, u32[]{:S(2)}) collective-permute-start(bf16[256,256]{1,0:T(8,128)(2,1)S(1)} %bitcast.22), channel_id=1, source_target_pairs={{0,0},{1,64},{64,128},{65,192},{128,1},{129,65},{192,129},{193,193... | collective-permute-start | bytes 393224 | tf_op jit(solution)/shard_map/ppermute | solution.py:242
  28.5 6.3 %collective-permute-start.2 = (bf16[256,256]{1,0:T(8,128)(2,1)S(1)}, bf16[256,256]{1,0:T(8,128)(2,1)S(1)}, u32[]{:S(2)}, u32[]{:S(2)}) collective-permute-start(bf16[256,256]{1,0:T(8,128)(2,1)S(1)} %bitcast.23), channel_id=1, source_target_pairs={{0,128},{1,192},{64,0},{65,64},{128,129},{129,193},{192,1},{193,65... | collective-permute-start | bytes 393224 | tf_op jit(solution)/shard_map/ppermute | solution.py:243
  35.4 1.6 collective-permute-start.4
  77.2 2.7 collective-permute-start.5
  119.7 4.4 %collective-permute-start.6 = (bf16[512,256]{1,0:T(8,128)(2,1)S(1)}, bf16[512,256]{1,0:T(8,128)(2,1)S(1)}, u32[]{:S(2)}, u32[]{:S(2)}) collective-permute-start(bf16[512,256]{1,0:T(8,128)(2,1)S(1)} %convolution_convert_fusion.1), channel_id=1, source_target_pairs={{0,1},{1,0},{2,3},{3,2},{4,5},{5,4},{6,7},{7,6},{8,9},{9,8},{10,11... | collective-permute-start | bytes 786440 | tf_op jit(solution)/shard_map/ppermute | solution.py:224
  158.8 2.5 collective-permute-start.7
  201.5 4.2 %collective-permute-start.8 = (bf16[512,256]{1,0:T(8,128)(2,1)S(1)}, bf16[512,256]{1,0:T(8,128)(2,1)S(1)}, u32[]{:S(2)}, u32[]{:S(2)}) collective-permute-start(bf16[512,256]{1,0:T(8,128)(2,1)S(1)} %convolution_convert_fusion), channel_id=1, source_target_pairs={{0,1},{1,0},{2,3},{3,2},{4,5},{5,4},{6,7},{7,6},{8,9},{9,8},{10,11... | collective-permute-start | bytes 786440 | tf_op jit(solution)/shard_map/ppermute | solution.py:224
  240.5 2.5 collective-permute-start.9
  260.7 15.4 %all-to-all-start.13 = ((f32[16,88,128]{2,1,0:T(8,128)}), f32[16,88,128]{2,1,0:T(8,128)S(1)}, u32[]{:S(2)}, u32[]{:S(2)}) async-start(f32[16,88,128]{2,1,0:T(8,128)} %broadcast_in_dim.27), calls=%async_computation.13 | async-start | bytes 1441792 | tf_op jit(solution)/shard_map/all_to_all | solution.py:216
  284.7 13.6 %all-to-all-start.14 = ((f32[16,1,256]{2,1,0:T(1,128)}), f32[16,1,256]{2,1,0:T(1,128)S(1)}, u32[]{:S(2)}, u32[]{:S(2)}) async-start(f32[16,1,256]{2,1,0:T(1,128)} %get-tuple-element.7), calls=%async_computation.14 | async-start | bytes 32768 | tf_op jit(solution)/shard_map/all_to_all | solution.py:261
  292.1 6.3 %collective-permute-start.11 = (f32[8,1024]{1,0:T(8,128)S(1)}, f32[8,1024]{1,0:T(8,128)S(1)}, u32[]{:S(2)}, u32[]{:S(2)}) collective-permute-start(f32[8,1024]{1,0:T(8,128)S(1)} %get-tuple-element.19), channel_id=1, source_target_pairs={{0,64},{1,192},{64,0},{65,128},{128,65},{129,193},{192,1},{193,129... | collective-permute-start | bytes 98312 | tf_op jit(solution)/shard_map/ppermute | solution.py:270
  292.6 6.7 %collective-permute-start.10 = (f32[8,1024]{1,0:T(8,128)S(1)}, f32[8,1024]{1,0:T(8,128)S(1)}, u32[]{:S(2)}, u32[]{:S(2)}) collective-permute-start(f32[8,1024]{1,0:T(8,128)S(1)} %get-tuple-element.20), channel_id=1, source_target_pairs={{0,0},{1,128},{64,64},{65,192},{128,1},{129,129},{192,65},{193,193... | collective-permute-start | bytes 98312 | tf_op jit(solution)/shard_map/ppermute | solution.py:270
